TPU v7x, 32 devices: a whole 2x2x4 slice. The times are simulated.
32 devices in a mesh: dp: 2 (over x), tp: 4 (over z), cp: 4 (over y, core).
Axes of the slice: x: 2, y: 2, z: 4, core: 2. Of those that a mesh axis runs over, the one named last changes fastest.
Arguments:
- hidden: bfloat16 [24, 24, 8192], P('dp'), parts along dimension 0
- attn_gain: bfloat16 [8192], replicated
- w_query: bfloat16 [8192, 8192], P(None, 'tp')
- w_key: bfloat16 [8192, 1024], P(None, 'tp')
- w_value: bfloat16 [8192, 1024], P(None, 'tp')
- w_out: bfloat16 [8192, 8192], P('tp')
- cache_k: bfloat16 [24, 4, 4, 8, 256, 128], P('dp', None, 'cp', 'tp'), parts along dimension 0
- cache_v: bfloat16 [24, 4, 4, 8, 256, 128], P('dp', None, 'cp', 'tp'), parts along dimension 0
- ctx_len: int32 [24], P('dp'), parts along dimension 0
- positions: int32 [24, 24], P('dp'), parts along dimension 0
- tree_mask: int32 [24, 24, 24], P('dp'), parts along dimension 0
Outputs:
- output 1: bfloat16 [24, 24, 8192], P('dp'), parts along dimension 0
- output 2: bfloat16 [24, 4, 4, 8, 256, 128], P('dp', None, 'cp', 'tp'), parts along dimension 0
- output 3: bfloat16 [24, 4, 4, 8, 256, 128], P('dp', None, 'cp', 'tp'), parts along dimension 0
There are 2 independent parts. A program takes and returns all parts, laid end to end along the dimension named above; an argument that names none is the same for every part.
All inputs are finite; a program needn't handle non-finite values.
Results may differ from a plain program's by a relative error of at most 0.00843603.
Values sent between devices are 32-bit elements.
A program may use at most 1 GiB of HBM per device.

v0:
```python
import math
import jax
import jax.numpy as jnp
from jax import lax
from jax.sharding import PartitionSpec as P

ROPE_THETA = 500000.0
NORM_EPS = 1e-5
MASKED = -1e30


def rope_tables(positions, head_dim):
    freq_idx = jnp.arange(head_dim // 2, dtype=jnp.float32)
    inv_freq = 1.0 / (ROPE_THETA ** (2.0 * freq_idx / head_dim))
    wavelen = 2.0 * math.pi / inv_freq
    smooth = (8192.0 / wavelen - 1.0) / 3.0
    blended = (1.0 - smooth) * inv_freq / 8.0 + smooth * inv_freq
    inv_freq = jnp.where(wavelen < 2048.0, inv_freq, jnp.where(wavelen > 8192.0, inv_freq / 8.0, blended))
    angle = positions.astype(jnp.float32)[..., None] * inv_freq
    return jnp.cos(angle)[..., None, :], jnp.sin(angle)[..., None, :]


def apply_rope(values, cos_tab, sin_tab):
    half = values.shape[-1] // 2
    first = values[..., :half]
    second = values[..., half:]
    return jnp.concatenate([first * cos_tab - second * sin_tab, second * cos_tab + first * sin_tab], axis=-1)


def rms_norm(hidden, attn_gain):
    wide = hidden.astype(jnp.float32)
    inv_rms = lax.rsqrt(jnp.mean(wide * wide, axis=-1, keepdims=True) + NORM_EPS)
    return wide, (wide * inv_rms * attn_gain.astype(jnp.float32)).astype(jnp.bfloat16)


def solution(mesh):
    cp_size = mesh.shape['cp']
    cache_spec = P('dp', None, 'cp', 'tp')
    row_spec = P('dp')

    def local_step(hidden, attn_gain, w_query, w_key, w_value, w_out, cache_k, cache_v, ctx_len, positions, tree_mask):
        num_reqs, tree_len, width = hidden.shape
        num_blocks = cache_k.shape[1]
        kv_local = cache_k.shape[3]
        blk_len = cache_k.shape[4]
        head_dim = cache_k.shape[5]
        heads_local = w_query.shape[1] // head_dim
        group = heads_local // kv_local
        cp_rank = lax.axis_index('cp')
        scale = head_dim ** -0.5
        wide, normed = rms_norm(hidden, attn_gain)
        flat_rows = normed.reshape(num_reqs * tree_len, width)
        query = jnp.dot(flat_rows, w_query, preferred_element_type=jnp.float32).reshape(num_reqs, tree_len, heads_local, head_dim)
        key_new = jnp.dot(flat_rows, w_key, preferred_element_type=jnp.float32).reshape(num_reqs, tree_len, kv_local, head_dim)
        val_new = jnp.dot(flat_rows, w_value, preferred_element_type=jnp.float32).astype(jnp.bfloat16).reshape(num_reqs, tree_len, kv_local, head_dim)
        cos_tab, sin_tab = rope_tables(positions, head_dim)
        query = apply_rope(query, cos_tab, sin_tab).astype(jnp.bfloat16).reshape(num_reqs, tree_len, kv_local, group, head_dim)
        key_new = apply_rope(key_new, cos_tab, sin_tab).astype(jnp.bfloat16)
        keys = cache_k[:, :, 0]
        values = cache_v[:, :, 0]
        score_cache = jnp.einsum('rtkgd,rjkid->rtkgji', query, keys, preferred_element_type=jnp.float32) * scale
        block_pos = (jnp.arange(num_blocks)[:, None] * cp_size + cp_rank) * blk_len + jnp.arange(blk_len)[None, :]
        valid = (block_pos[None] < ctx_len[:, None, None])[:, None, None, None]
        score_tree = jnp.einsum('rtkgd,rskd->rtkgs', query, key_new, preferred_element_type=jnp.float32) * scale
        tree_ok = ((tree_mask > 0) & (cp_rank == 0))[:, :, None, None, :]
        score_cache = jnp.where(valid, score_cache, MASKED)
        score_tree = jnp.where(tree_ok, score_tree, MASKED)
        row_max = jnp.maximum(score_cache.max(axis=(4, 5)), score_tree.max(axis=-1))
        prob_cache = jnp.where(valid, jnp.exp(score_cache - row_max[..., None, None]), 0.0)
        prob_tree = jnp.where(tree_ok, jnp.exp(score_tree - row_max[..., None]), 0.0)
        row_sum = prob_cache.sum(axis=(4, 5)) + prob_tree.sum(axis=-1)
        out_part = jnp.einsum('rtkgji,rjkid->rtkgd', prob_cache.astype(jnp.bfloat16), values, preferred_element_type=jnp.float32)
        out_part = out_part + jnp.einsum('rtkgs,rskd->rtkgd', prob_tree.astype(jnp.bfloat16), val_new, preferred_element_type=jnp.float32)
        glob_max = lax.pmax(row_max, 'cp')
        factor = jnp.exp(row_max - glob_max)
        glob_sum = lax.psum(row_sum * factor, 'cp')
        glob_out = lax.psum(out_part * factor[..., None], 'cp')
        attn_out = (glob_out / glob_sum[..., None]).astype(jnp.bfloat16).reshape(num_reqs, tree_len, heads_local * head_dim)
        proj_part = jnp.einsum('rtf,fe->rte', attn_out, w_out, preferred_element_type=jnp.float32).astype(jnp.bfloat16)
        proj_sum = lax.psum(proj_part.astype(jnp.float32), 'tp')
        out_hidden = (wide + proj_sum).astype(jnp.bfloat16)
        slot_ids = ctx_len[:, None] + jnp.arange(tree_len)[None, :]
        block_ids = slot_ids // blk_len
        local_blk = jnp.where(block_ids % cp_size == cp_rank, block_ids // cp_size, num_blocks)
        req_ids = jnp.broadcast_to(jnp.arange(num_reqs)[:, None], (num_reqs, tree_len))
        new_keys = keys.at[req_ids, local_blk, :, slot_ids % blk_len, :].set(key_new, mode='drop')
        new_vals = values.at[req_ids, local_blk, :, slot_ids % blk_len, :].set(val_new, mode='drop')
        return out_hidden, new_keys[:, :, None], new_vals[:, :, None]

    program = jax.shard_map(local_step, mesh=mesh, in_specs=(row_spec, P(), P(None, 'tp'), P(None, 'tp'), P(None, 'tp'), P('tp', None), cache_spec, cache_spec, row_spec, row_spec, row_spec), out_specs=(row_spec, cache_spec, cache_spec), check_vma=False)
    return program
```

profile of v0, /device:TPU:0, one launch (start us, length us, event | category | flops | bytes accessed | tf_op | source)
XLA Modules:
  0.0 596.9 jit_solution(1537434838746617109)
XLA Ops:
  7.2 0.7 convert_element_type.37
  8.0 3.4 fusion.12
  11.3 40.4 %copy.96 = bf16[2048,8192]{1,0:T(8,128)(2,1)} copy(bf16[2048,8192]{0,1:T(8,128)(2,1)} %bitcast.99) | data formatting | bytes 67108864 | tf_op jit(solution)/shard_map/dot_general | solution.py:53
  51.8 3.7 fusion.14
  55.5 17.0 %fusion.25 = f32[12,24,16,128]{3,1,2,0:T(8,128)S(1)} fusion(bf16[16,128,8192,1]{2,1,0,3:T(8,128)(2,1)} %bitcast.100, bf16[12,24,8192]{2,1,0:T(8,128)(2,1)S(1)} %fusion.14), kind=kOutput, calls=%fused_computation.28 | convolution fusion | flops 9663676416 | bytes 40632320 | tf_op jit(solution)/shard_map/dot_general | solution.py:53
  72.5 0.6 multiply_cosine_fusion
  73.1 0.9 subtract_convert_fusion
  74.1 0.2 copy.70
  74.3 0.2 copy.71
  74.5 6.3 %copy.99 = bf16[256,8192]{1,0:T(8,128)(2,1)} copy(bf16[256,8192]{0,1:T(8,128)(2,1)} %bitcast.107) | data formatting | bytes 8388608 | tf_op jit(solution)/shard_map/dot_general | solution.py:54
  80.9 5.9 fusion.23
  86.7 0.9 subtract_convert_fusion.1
  87.6 0.7 copy.74
  88.4 0.7 pad_maximum_fusion
  89.0 1.1 pad_maximum_fusion.1
  90.1 0.6 copy-done.4
  90.8 3.5 fusion.28
  94.2 1.8 copy.77
  96.1 11.8 %copy.121 = bf16[12,4,1,2,256,128]{5,3,4,1,0,2:T(2,128)(2,1)S(1)} copy(bf16[12,4,1,2,256,128]{5,4,3,2,1,0:T(8,128)(2,1)} %param.17) | data formatting | bytes 12582912 | tf_op args[6]
  107.9 0.1 broadcast_compare_fusion
  108.0 8.4 %bitcast_reduce_fusion = (f32[12,24,2,8]{3,1,2,0:T(8,128)S(1)}, f32[12,2,24,8,4,256]{5,3,4,2,1,0:T(8,128)}) fusion(pred[12,4,256]{2,1,0:T(4,128)(4,1)S(1)} %broadcast_compare_fusion, bf16[12,4,2,256,128,1]{4,2,3,1,0,5:T(2,128)(2,1)S(1)} %bitcast.96, bf16[12,24,2,8,128]{4,3,1,2,0:T(8,128)(2,1)S(1)} %pad_maximum_fusion), kind=kOutput, calls=%fused_computation.5 | convolution fusion | flops 1222110720 | bytes 26376192 | tf_op jit(solution)/shard_map/rtkgd,rjkid->rtkgji/dot_general | solution.py:61
  116.5 0.1 copy.80
  116.6 16.8 %pmax.7 = f32[12,24,2,8]{3,1,2,0:T(8,128)} all-reduce(f32[12,24,2,8]{3,1,2,0:T(8,128)S(1)} %max.13), channel_id=1, replica_groups=mesh['dp'=2,'tp'=4,'cp'=4] {'cp'}, use_global_device_ids=true, to_apply=%region_3.4 | all-reduce | flops 4608 | bytes 36864 | tf_op jit(solution)/shard_map/pmax | solution.py:74
  133.4 2.6 fusion.29
  136.0 0.1 copy.83
  136.2 9.1 %fusion.4 = f32[12,24,2,8]{3,1,2,0:T(8,128)S(1)} fusion(f32[12,2,24,8,4,256]{5,3,4,2,1,0:T(8,128)} %get-tuple-element.30, f32[12,24,2,8]{3,1,2,0:T(8,128)S(1)} %max.13, pred[12,4,256]{2,1,0:T(4,128)(4,1)S(1)} %broadcast_compare_fusion), kind=kLoop, calls=%fused_computation.12 | loop fusion | flops 23588352 | bytes 18923520 | tf_op jit(solution)/shard_map/reduce_sum | solution.py:71
  145.2 0.9 copy.82
  146.1 11.8 %copy.120 = bf16[12,4,1,2,256,128]{5,3,4,1,0,2:T(2,128)(2,1)S(1)} copy(bf16[12,4,1,2,256,128]{5,4,3,2,1,0:T(8,128)(2,1)} %param.18) | data formatting | bytes 12582912 | tf_op args[7]
  157.9 12.0 %fusion.16 = f32[12,2,24,8,128,1]{4,3,5,2,1,0:T(8,128)} fusion(f32[12,2,24,8,4,256]{5,3,4,2,1,0:T(8,128)} %get-tuple-element.30, f32[12,24,2,8]{3,1,2,0:T(8,128)S(1)} %max.13, pred[12,4,256]{2,1,0:T(4,128)(4,1)S(1)} %broadcast_compare_fusion, bf16[12,4,2,256,128,1]{4,2,3,1,0,5:T(2,128)(2,1)S(1)} %bitcast.101), kind=kOutput, calls=%fused_computation.20 | convolution fusion | flops 1231552512 | bytes 27555840 | tf_op jit(solution)/shard_map/rtkgji,rjkid->rtkgd/dot_general | solution.py:72
  170.0 5.0 convolution_convert_fusion
  175.1 0.1 add_multiply_fusion
  175.2 3.1 fusion.27
  178.4 16.6 %psum.22 = f32[12,24,2,8]{3,1,2,0:T(8,128)S(1)} all-reduce(f32[12,24,2,8]{3,1,2,0:T(8,128)S(1)} %get-tuple-element.15), channel_id=1, replica_groups=mesh['dp'=2,'tp'=4,'cp'=4] {'cp'}, use_global_device_ids=true, to_apply=%region_7.8 | all-reduce | flops 4608 | bytes 36864 | tf_op jit(solution)/shard_map/psum | solution.py:76
  195.0 42.8 %all-reduce.3.cloned.1.call-done = f32[12,24,2,8,128]{4,3,1,2,0:T(8,128)} async-done(((f32[12,24,2,8,128]{4,3,1,2,0:T(8,128)}), f32[12,24,2,8,128]{4,3,1,2,0:T(8,128)}) %all-reduce.3.cloned.1.call-update) | async-done | bytes 2359312 | tf_op jit(solution)/shard_map/psum | solution.py:77
  237.8 2.1 divide_convert_fusion
  239.8 0.2 copy.84
  240.1 0.5 reshape.326
  240.6 18.1 %fusion.9 = f32[12,24,8192]{2,1,0:T(8,128)} fusion(bf16[12,24,2048]{2,1,0:T(8,128)(2,1)S(1)} %reshape.326, bf16[2048,8192]{1,0:T(8,128)(2,1)} %param.16), kind=kOutput, calls=%fused_computation.15 | convolution fusion | flops 9668395008 | bytes 44171264 | tf_op jit(solution)/shard_map/rtf,fe->rte/dot_general | solution.py:79
  258.7 0.9 copy-done.5
  259.6 0.1 copy.86
  259.8 0.1 fusion.39
  259.9 0.1 reshape.327
  259.9 37.1 %scatter_fusion = bf16[12,4,2,256,128]{4,2,3,1,0:T(2,128)(2,1)} fusion(bf16[12,4,2,256,128]{4,2,3,1,0:T(2,128)(2,1)} %bitcast.97, s32[288]{0:T(512)S(1)} %reshape.327, bf16[288,2,128]{2,1,0:T(2,128)(2,1)S(1)} %copy.86), kind=kCustom, calls=%fused_computation | custom fusion | bytes 445824 | tf_op jit(solution)/shard_map/scatter | solution.py:86
  297.1 7.2 %copy.87 = bf16[12,4,1,2,256,128]{5,4,3,2,1,0:T(8,128)(2,1)} copy(bf16[12,4,1,2,256,128]{5,3,4,1,0,2:T(2,128)(2,1)} %bitcast.98) | data formatting | bytes 12582912
  304.2 36.7 %scatter_fusion.1 = bf16[12,4,2,256,128]{4,2,3,1,0:T(2,128)(2,1)} fusion(bf16[12,4,2,256,128]{4,2,3,1,0:T(2,128)(2,1)} %bitcast.102, s32[288]{0:T(512)S(1)} %reshape.327, bf16[288,2,128]{2,1,0:T(2,128)(2,1)S(1)} %reshape.335), kind=kCustom, calls=%fused_computation.1 | custom fusion | bytes 445824 | tf_op jit(solution)/shard_map/scatter | solution.py:87
  340.9 7.2 %copy.88 = bf16[12,4,1,2,256,128]{5,4,3,2,1,0:T(8,128)(2,1)} copy(bf16[12,4,1,2,256,128]{5,3,4,1,0,2:T(2,128)(2,1)} %bitcast.103) | data formatting | bytes 12582912
  348.1 233.5 %all-reduce.5.cloned.1.call-done = f32[12,24,8192]{2,1,0:T(8,128)} async-done(((f32[12,24,8192]{2,1,0:T(8,128)}), f32[12,24,8192]{2,1,0:T(8,128)}) %all-reduce.5.cloned.1.call-update) | async-done | bytes 9437200 | tf_op jit(solution)/shard_map/psum | solution.py:80
  581.5 8.5 %fusion.15 = bf16[12,24,8192]{2,1,0:T(8,128)(2,1)} fusion(f32[12,24,8192]{2,1,0:T(8,128)} %all-reduce.5.cloned.1.call-done, bf16[12,24,8192]{2,1,0:T(8,128)(2,1)} %param.11), kind=kLoop, calls=%fused_computation.19 | loop fusion | flops 7077888 | bytes 18874368 | tf_op jit(solution)/shard_map/convert_element_type | solution.py:81
  (34 shorter events, 0.4 us)
Async XLA Ops:
  7.2 230.6 %all-reduce.3.cloned.1.call-start = ((), (), s32[]{:S(2)}) async-start(), calls=%async_computation | async-start | bytes 4718592 | tf_op jit(solution)/shard_map/psum | solution.py:77
  11.3 40.4 %copy-start.9 = (s32[12,24]{1,0:T(8,128)S(1)}, s32[12,24]{1,0:T(8,128)}, u32[]{:S(2)}) copy-start(s32[12,24]{1,0:T(8,128)} %param.20) | copy-start | bytes 3460
  55.5 17.0 %copy-start.2 = (bf16[12,24,8192]{2,1,0:T(8,128)(2,1)}, bf16[12,24,8192]{2,1,0:T(8,128)(2,1)S(1)}, u32[]{:S(2)}) copy-start(bf16[12,24,8192]{2,1,0:T(8,128)(2,1)S(1)} %fusion.14) | copy-start | bytes 14155780
  80.9 6.7 %copy-start.8 = (s32[12,24,24]{2,1,0:T(8,128)S(1)}, s32[12,24,24]{2,1,0:T(8,128)}, u32[]{:S(2)}) copy-start(s32[12,24,24]{2,1,0:T(8,128)} %param.21) | copy-start | bytes 82948
  90.1 0.7 copy-start.4
  96.1 11.8 %copy-start.10 = (s32[12]{0:T(128)S(1)}, s32[12]{0:T(128)}, u32[]{:S(2)}) copy-start(s32[12]{0:T(128)} %param.19) | copy-start | bytes 148
  107.9 8.5 %copy-start = (bf16[12,4,1,2,256,128]{5,3,4,1,0,2:T(2,128)(2,1)}, bf16[12,4,1,2,256,128]{5,3,4,1,0,2:T(2,128)(2,1)S(1)}, u32[]{:S(2)}) copy-start(bf16[12,4,1,2,256,128]{5,3,4,1,0,2:T(2,128)(2,1)S(1)} %copy.121) | copy-start | bytes 18874372
  108.0 8.4 %copy-start.7 = (f32[12,24,2,8]{3,1,2,0:T(8,128)S(1)}, f32[12,24,2,8]{3,1,2,0:T(8,128)}, u32[]{:S(2)}) copy-start(f32[12,24,2,8]{3,1,2,0:T(8,128)} %copy.77) | copy-start | bytes 55300
  136.1 9.1 %copy-start.3 = (bf16[12,24,2,8,24]{1,4,3,2,0:T(8,128)(2,1)S(1)}, bf16[12,24,2,8,24]{1,4,3,2,0:T(8,128)(2,1)}, u32[]{:S(2)}) copy-start(bf16[12,24,2,8,24]{1,4,3,2,0:T(8,128)(2,1)} %get-tuple-element.24) | copy-start | bytes 663556
  157.9 12.1 %copy-start.1 = (bf16[12,4,1,2,256,128]{5,3,4,1,0,2:T(2,128)(2,1)}, bf16[12,4,1,2,256,128]{5,3,4,1,0,2:T(2,128)(2,1)S(1)}, u32[]{:S(2)}) copy-start(bf16[12,4,1,2,256,128]{5,3,4,1,0,2:T(2,128)(2,1)S(1)} %copy.120) | copy-start | bytes 18874372
  170.0 5.1 copy-start.6
  178.3 403.2 %all-reduce.5.cloned.1.call-start = ((), (), s32[]{:S(2)}) async-start(), calls=%async_computation.1 | async-start | bytes 18874368 | tf_op jit(solution)/shard_map/psum | solution.py:80
  258.7 0.9 copy-start.5
Sparse Core Ops, SparseCore 0:
  178.4 59.2 all-reduce.2
  258.8 322.6 all-reduce.4
where the time goes:
time: 599 us; the launch traced here: 597 us
  waiting for transfers between devices  276 us (46%)
  local copies, waits for them, and re-layouts  165 us (28%)
  matrix products  73 us (12%)
  other arithmetic  34.6 us (6%)
  blocking collectives  33.4 us (6%)
  between operations  14.3 us (2%)
    psum x1, waiting for transfers between devices, local_step(): proj_sum = lax.psum(proj_part.astype(jnp.float32), 'tp')  233 us
    psum x1, waiting for transfers between devices, local_step(): glob_out = lax.psum(out_part * factor[..., None], 'cp')  42.8 us
    dot_general x1, local copies, waits for them, and re-layouts, local_step(): jnp.dot(flat_rows, w_query, preferred_element_type=jnp.float32)  40.4 us
    unnamed x26, local copies, waits for them, and re-layouts  39.5 us
    scatter x1, local copies, waits for them, and re-layouts, local_step(): keys.at[req_ids, local_blk, :, slot_ids % blk_len, :]  37.1 us
    scatter x1, local copies, waits for them, and re-layouts, local_step(): values.at[req_ids, local_blk, :, slot_ids % blk_len, :]  36.7 us
    dot_general x1, matrix products, local_step(): jnp.einsum('rtf,fe->rte', attn_out, w_out, preferred_element_type=jnp.flo...  18.1 us
    dot_general x1, matrix products, local_step(): jnp.dot(flat_rows, w_query, preferred_element_type=jnp.float32)  17 us
  transfers between devices with their start and end apart: 2, of which 2 were waited for; matrix products, arithmetic and copies ran while one was open for 15% of the time, Pallas kernels for 0%

commit v1 on v0

v1 whole, which is shorter than its diff:
```python
import math
import jax
import jax.numpy as jnp
from jax import lax
from jax.experimental import pallas as pl
from jax.experimental.pallas import tpu as pltpu
from jax.sharding import PartitionSpec as P

ROPE_THETA = 500000.0
NORM_EPS = 1e-5
MASKED = -1e30
LOG2E = 1.4426950408889634
MESH = pl.DeviceIdType.MESH

REQ = 12
TREE = 24
ROWS = REQ * TREE
D = 8192
HEAD = 128
KV = 2
GROUP = 8
HEADS = KV * GROUP
NBLK = 4
BLK = 256
CP = 4
WIDE = HEADS * HEAD
EXT = WIDE + HEAD
TILE = 256
NTILE = (HEADS + 2 * KV) * HEAD // TILE
RING = 4
HALF = D // 2
MINE = ROWS // 2
NP = 16
W = HALF // NP


def rope_tables(positions):
    freq_idx = jnp.arange(HEAD // 2, dtype=jnp.float32)
    inv_freq = 1.0 / (ROPE_THETA ** (2.0 * freq_idx / HEAD))
    wavelen = 2.0 * math.pi / inv_freq
    smooth = (8192.0 / wavelen - 1.0) / 3.0
    blended = (1.0 - smooth) * inv_freq / 8.0 + smooth * inv_freq
    inv_freq = jnp.where(wavelen < 2048.0, inv_freq, jnp.where(wavelen > 8192.0, inv_freq / 8.0, blended))
    angle = positions.astype(jnp.float32).reshape(ROWS, 1) * inv_freq
    cos_tab, sin_tab = jnp.cos(angle), jnp.sin(angle)
    return jnp.concatenate([cos_tab, cos_tab], axis=-1), jnp.concatenate([-sin_tab, sin_tab], axis=-1)


def attend_kernel(ctx_ref, gain_ref, cos_ref, sin_ref, mask_ref, x_hbm, wq_hbm, wk_hbm, wv_hbm, ck_hbm, cv_hbm,
                  o_hbm, nk_hbm, nv_hbm,
                  x_ref, h_ref, wbuf, qkv, kbuf, vbuf, obuf, xsem, wsem, ksem, vsem, nksem, nvsem, osem):
    cp_rank = lax.axis_index('cp')
    nq = HEADS * HEAD // TILE

    x_copy = pltpu.make_async_copy(x_hbm, x_ref, xsem)
    x_copy.start()

    def start_weight(i):
        slot = lax.rem(i, RING)

        @pl.when(i < nq)
        def _():
            cols = pl.ds(pl.multiple_of(i * TILE, TILE), TILE)
            pltpu.make_async_copy(wq_hbm.at[:, cols], wbuf.at[slot], wsem.at[slot]).start()

        @pl.when(i == nq)
        def _():
            pltpu.make_async_copy(wk_hbm, wbuf.at[slot], wsem.at[slot]).start()

        @pl.when(i == nq + 1)
        def _():
            pltpu.make_async_copy(wv_hbm, wbuf.at[slot], wsem.at[slot]).start()

    def start_cache(r):
        pltpu.make_async_copy(ck_hbm.at[r, :, 0], kbuf.at[r], ksem.at[r]).start()
        pltpu.make_async_copy(cv_hbm.at[r, :, 0], vbuf.at[r], vsem.at[r]).start()

    for i in range(RING):
        start_weight(jnp.int32(i))
    x_copy.wait()

    def norm_step(i, carry):
        rows = pl.ds(pl.multiple_of(i * 16, 16), 16)
        wide = x_ref[rows, :].astype(jnp.float32)
        inv = lax.rsqrt(jnp.mean(wide * wide, axis=-1, keepdims=True) + NORM_EPS)
        h_ref[rows, :] = (wide * inv * gain_ref[...].astype(jnp.float32)).astype(jnp.bfloat16)
        return carry

    lax.fori_loop(0, ROWS // 16, norm_step, 0)

    def proj_step(i, carry):
        slot = lax.rem(i, RING)
        pltpu.make_async_copy(wk_hbm, wbuf.at[slot], wsem.at[slot]).wait()
        acc = jnp.dot(h_ref[...], wbuf[slot], preferred_element_type=jnp.float32)
        for hh in range(TILE // HEAD):
            part = acc[:, hh * HEAD:(hh + 1) * HEAD]
            turned = pltpu.roll(part, HEAD // 2, 1)
            cos_tab = jnp.where(i < NTILE - 1, cos_ref[...], 1.0)
            sin_tab = jnp.where(i < NTILE - 1, sin_ref[...], 0.0)
            qkv[(TILE // HEAD) * i + hh] = part * cos_tab + turned * sin_tab

        @pl.when(i + RING < NTILE)
        def _():
            start_weight(i + RING)

        @pl.when(i + RING >= NTILE)
        def _():
            start_cache(i + RING - NTILE)
        return carry

    lax.fori_loop(0, NTILE, proj_step, 0)

    def attend_step(r, carry):
        @pl.when(r + RING < REQ)
        def _():
            start_cache(r + RING)

        pltpu.make_async_copy(ck_hbm.at[r, :, 0], kbuf.at[r], ksem.at[r]).wait()
        pltpu.make_async_copy(cv_hbm.at[r, :, 0], vbuf.at[r], vsem.at[r]).wait()
        ctx = ctx_ref[r]
        rows = pl.ds(pl.multiple_of(r * TREE, 8), TREE)
        first = ctx // BLK
        last = (ctx + TREE - 1) // BLK

        def insert(block):
            j = block // CP
            slot_of = lax.broadcasted_iota(jnp.int32, (BLK, TREE), 0) + (block * BLK - ctx)
            pick = (slot_of == lax.broadcasted_iota(jnp.int32, (BLK, TREE), 1)).astype(jnp.bfloat16)
            wide_slot = lax.broadcasted_iota(jnp.int32, (BLK, HEAD), 0) + (block * BLK - ctx)
            inside = (wide_slot >= 0) & (wide_slot < TREE)
            for hd in range(KV):
                for buf, base in ((kbuf, HEADS), (vbuf, HEADS + KV)):
                    new = qkv[base + hd, rows, :].astype(jnp.bfloat16)
                    placed = jnp.dot(pick, new, preferred_element_type=jnp.float32)
                    old = buf[r, j, hd].astype(jnp.float32)
                    buf[r, j, hd] = jnp.where(inside, placed, old).astype(jnp.bfloat16)

        @pl.when(lax.rem(first, CP) == cp_rank)
        def _():
            insert(first)

        @pl.when((lax.rem(last, CP) == cp_rank) & (last != first))
        def _():
            insert(last)

        pltpu.make_async_copy(kbuf.at[r], nk_hbm.at[r, :, 0], nksem.at[r]).start()
        pltpu.make_async_copy(vbuf.at[r], nv_hbm.at[r, :, 0], nvsem.at[r]).start()

        lane = lax.broadcasted_iota(jnp.int32, (TREE, NBLK * BLK), 1)
        pos = (lane // BLK * CP + cp_rank) * BLK + lane % BLK - ctx
        onehot = (pos == lax.broadcasted_iota(jnp.int32, (TREE, NBLK * BLK), 0)).astype(jnp.bfloat16)
        allowed = jnp.dot(mask_ref[r].astype(jnp.float32).astype(jnp.bfloat16), onehot, preferred_element_type=jnp.float32)
        bias = jnp.where((pos < 0) | (allowed > 0.5), 0.0, MASKED)

        stats = jnp.zeros((TREE, HEAD), jnp.float32)
        stat_lane = lax.broadcasted_iota(jnp.int32, (TREE, HEAD), 1)
        for hd in range(KV):
            query = qkv[hd * GROUP:(hd + 1) * GROUP, rows, :].reshape(GROUP * TREE, HEAD).astype(jnp.bfloat16)
            keys = kbuf[r, :, hd].reshape(NBLK * BLK, HEAD)
            vals = vbuf[r, :, hd].reshape(NBLK * BLK, HEAD)
            score = lax.dot_general(query, keys, (((1,), (1,)), ((), ())), preferred_element_type=jnp.float32)
            score = score.reshape(GROUP, TREE, NBLK * BLK) * (HEAD ** -0.5 * LOG2E) + bias[None]
            top = jnp.max(score, axis=-1, keepdims=True)
            prob = jnp.exp2(score - top)
            total = jnp.sum(prob, axis=-1, keepdims=True)
            mixed = jnp.dot(prob.reshape(GROUP * TREE, NBLK * BLK).astype(jnp.bfloat16), vals, preferred_element_type=jnp.float32)
            for g in range(GROUP):
                head = hd * GROUP + g
                obuf[r, :, head * HEAD:(head + 1) * HEAD] = mixed[g * TREE:(g + 1) * TREE]
                stats = jnp.where(stat_lane == head, top[g], stats)
                stats = jnp.where(stat_lane == HEADS + head, total[g], stats)
        obuf[r, :, WIDE:] = stats
        pltpu.make_async_copy(obuf.at[r], o_hbm.at[r], osem.at[r]).start()
        return carry

    lax.fori_loop(0, REQ, attend_step, 0)

    def drain(r, carry):
        pltpu.make_async_copy(kbuf.at[r], nk_hbm.at[r, :, 0], nksem.at[r]).wait()
        pltpu.make_async_copy(vbuf.at[r], nv_hbm.at[r, :, 0], nvsem.at[r]).wait()
        pltpu.make_async_copy(obuf.at[r], o_hbm.at[r], osem.at[r]).wait()
        return carry

    lax.fori_loop(0, REQ, drain, 0)


def merge(a, b):
    ta, tb = a[:, WIDE:], b[:, WIDE:]
    top = jnp.maximum(ta, tb)
    fa, fb = jnp.exp2(ta - top), jnp.exp2(tb - top)
    total = ta * pltpu.roll(fa, HEADS, 1) + tb * pltpu.roll(fb, HEADS, 1)
    lane = lax.broadcasted_iota(jnp.int32, (TREE, HEAD), 1)
    return fa, fb, top, total, jnp.where(lane < HEADS, top, total)


def tail_kernel(o_hbm, w_hbm, x_hbm, y_ref,
                own, pin, ysend, yrecv, keep, heads, hbf, wbuf, xbuf,
                part, in_end, in_mid, fin, fin_y, fin_c, fin_cy,
                osem, wsem, xsem, s_p, r_p, s_y, r_y, s_a, r_a,
                s_e, r_e, s_m, r_m, s_f, r_f, s_yf, r_yf, s_cf, r_cf, s_cy, r_cy):
    cp_rank = lax.axis_index('cp')
    z = lax.axis_index('tp')
    yy = cp_rank // 2
    core = cp_rank % 2
    other_core = 1 - core
    other_y = 1 - yy
    mid = (z + 1) // 2 % 2
    partner = {'cp': yy * 2 + other_core}
    across = {'cp': other_y * 2 + core}
    pair = {'tp': z + 1 - 2 * (z % 2)}
    middle = {'tp': 3 - z}

    def remote(src, dst, send, recv, peer):
        return pltpu.make_async_remote_copy(src_ref=src, dst_ref=dst, send_sem=send, recv_sem=recv, device_id=peer, device_id_type=MESH)

    own_copies = [pltpu.make_async_copy(o_hbm.at[r], own.at[r], osem.at[r]) for r in range(REQ)]
    for copy in own_copies:
        copy.start()

    def weight_copy(j):
        cols = pl.ds(pl.multiple_of(core * HALF + j * W, W), W)
        return pltpu.make_async_copy(w_hbm.at[:, cols], wbuf.at[j], wsem.at[j])

    def start_weight(j, carry):
        weight_copy(j).start()
        return carry

    lax.fori_loop(0, NP, start_weight, 0)
    x_copy = pltpu.make_async_copy(
        x_hbm.at[pl.ds(pl.multiple_of(yy * MINE, 16), MINE), pl.ds(pl.multiple_of(core * HALF, HALF), HALF)], xbuf, xsem)
    x_copy.start()

    barrier = pltpu.get_barrier_semaphore()
    for peer in (partner, across, pair):
        pl.semaphore_signal(barrier, inc=1, device_id=peer, device_id_type=MESH)

    @pl.when(mid == 1)
    def _():
        pl.semaphore_signal(barrier, inc=1, device_id=middle, device_id_type=MESH)
        pl.semaphore_wait(barrier, 4)

    @pl.when(mid == 0)
    def _():
        pl.semaphore_wait(barrier, 3)

    for copy in own_copies:
        copy.wait()

    def chip_copy(side, q):
        chip = yy if side else other_y
        return remote(own.at[6 * chip + 3 * other_core + q], pin.at[3 * side + q], s_p.at[3 * side + q], r_p.at[3 * side + q], partner)

    for side in (0, 1):
        for q in range(3):
            chip_copy(side, q).start()

    def y_copy(q):
        return remote(ysend.at[q], yrecv.at[q], s_y.at[q], r_y.at[q], across)

    def blend(a, b, out):
        fa, fb, top, total, stats = merge(a, b)
        for h in range(HEADS):
            cols = slice(h * HEAD, (h + 1) * HEAD)
            out[:, cols] = a[:, cols] * fa[:, h:h + 1] + b[:, cols] * fb[:, h:h + 1]
        out[:, WIDE:] = stats

    for q in range(3):
        chip_copy(0, q).wait_recv()
        blend(own.at[6 * other_y + 3 * core + q], pin.at[q], ysend.at[q])
        y_copy(q).start()
    for q in range(3):
        chip_copy(1, q).wait_recv()
        blend(own.at[6 * yy + 3 * core + q], pin.at[3 + q], keep.at[q])

    def head_copy(q, owner):
        slot = 3 * owner + q
        return remote(heads.at[slot], heads.at[slot], s_a.at[q], r_a.at[q], partner)

    for q in range(3):
        y_copy(q).wait_recv()
        a, b, out = keep.at[q], yrecv.at[q], heads.at[3 * core + q]
        fa, fb, top, total, stats = merge(a, b)
        inv = 1.0 / total
        for h in range(HEADS):
            cols = slice(h * HEAD, (h + 1) * HEAD)
            mixed = a[:, cols] * fa[:, h:h + 1] + b[:, cols] * fb[:, h:h + 1]
            out[:, cols] = mixed * inv[:, HEADS + h:HEADS + h + 1]
        head_copy(q, core).start()
    for q in range(3):
        head_copy(q, other_core).wait_recv()
    hbf[...] = heads[...].reshape(MINE, WIDE).astype(jnp.bfloat16)

    def end_copy(j):
        return remote(part.at[j], in_end.at[j], s_e.at[j], r_e.at[j], pair)

    def mid_copy(j):
        return remote(part.at[j], in_mid.at[j], s_m.at[j], r_m.at[j], middle)

    def fin_copy(j):
        return remote(fin.at[j], fin.at[j], s_f.at[j], r_f.at[j], pair)

    def across_copy(j):
        return remote(fin.at[j], fin_y.at[j], s_yf.at[j], r_yf.at[j], across)

    def core_copy(j):
        return remote(fin.at[j], fin_c.at[j], s_cf.at[j], r_cf.at[j], partner)

    def core_y_copy(j):
        return remote(fin_y.at[j], fin_cy.at[j], s_cy.at[j], r_cy.at[j], partner)

    def project(j, carry):
        weight_copy(j).wait()
        prod = jnp.dot(hbf[...], wbuf[j], preferred_element_type=jnp.float32)
        part[j] = prod.astype(jnp.bfloat16).astype(jnp.float32)

        @pl.when(mid == 0)
        def _():
            end_copy(j).start()
        return carry

    lax.fori_loop(0, NP, project, 0)
    x_copy.wait()

    def emit(buf, j, chip, half):
        rows = pl.ds(pl.multiple_of(chip * MINE, 16), MINE)
        cols = pl.ds(pl.multiple_of(half * HALF + j * W, W), W)
        y_ref[rows, cols] = buf[j].astype(jnp.bfloat16)

    def staged(s, lag, body):
        j = s - lag

        @pl.when((j >= 0) & (j < NP))
        def _():
            body(j)

    def take_end(j):
        end_copy(j).wait_recv()
        part[j] = part[j] + in_end[j]
        mid_copy(j).start()

    def take_mid(j):
        mid_copy(j).wait_recv()
        xcols = pl.ds(pl.multiple_of(j * W, W), W)
        fin[j] = (part[j] + in_mid[j]) + xbuf[:, xcols].astype(jnp.float32)
        fin_copy(j).start()
        across_copy(j).start()
        core_copy(j).start()
        emit(fin, j, yy, core)

    def take_fin(j):
        fin_copy(j).wait_recv()
        across_copy(j).start()
        core_copy(j).start()
        emit(fin, j, yy, core)

    def take_core(j):
        core_copy(j).wait_recv()
        emit(fin_c, j, yy, other_core)

    def take_across(j):
        across_copy(j).wait_recv()
        core_y_copy(j).start()
        emit(fin_y, j, other_y, core)

    def take_core_y(j):
        core_y_copy(j).wait_recv()
        emit(fin_cy, j, other_y, other_core)

    @pl.when(mid == 1)
    def _():
        def step(s, carry):
            staged(s, 0, take_end)
            staged(s, 1, take_mid)
            staged(s, 2, take_core)
            staged(s, 4, take_across)
            staged(s, 5, take_core_y)
            return carry

        lax.fori_loop(0, NP + 5, step, 0)

    @pl.when(mid == 0)
    def _():
        def step(s, carry):
            staged(s, 0, take_fin)
            staged(s, 1, take_core)
            staged(s, 2, take_across)
            staged(s, 3, take_core_y)
            return carry

        lax.fori_loop(0, NP + 3, step, 0)

    for side in (0, 1):
        for q in range(3):
            chip_copy(side, q).wait_send()
    for q in range(3):
        y_copy(q).wait_send()
        head_copy(q, core).wait_send()

    def sent(j, carry):
        across_copy(j).wait_send()
        core_copy(j).wait_send()
        core_y_copy(j).wait_send()

        @pl.when(mid == 1)
        def _():
            mid_copy(j).wait_send()
            fin_copy(j).wait_send()

        @pl.when(mid == 0)
        def _():
            end_copy(j).wait_send()
        return carry

    lax.fori_loop(0, NP, sent, 0)


def solution(mesh):
    cache_spec = P('dp', None, 'cp', 'tp')
    row_spec = P('dp')
    anywhere = pl.BlockSpec(memory_space=pl.ANY)
    vmem = pl.BlockSpec(memory_space=pltpu.VMEM)
    smem = pl.BlockSpec(memory_space=pltpu.SMEM)
    dma = pltpu.SemaphoreType.DMA
    f32, bf16 = jnp.float32, jnp.bfloat16

    def local_step(hidden, attn_gain, w_query, w_key, w_value, w_out, cache_k, cache_v, ctx_len, positions, tree_mask):
        cos_tab, sin_tab = rope_tables(positions)
        flat = hidden.reshape(ROWS, D)
        cache_shape = jax.ShapeDtypeStruct(cache_k.shape, bf16)
        partial_out, new_k, new_v = pl.pallas_call(
            attend_kernel,
            out_shape=(jax.ShapeDtypeStruct((REQ, TREE, EXT), f32), cache_shape, cache_shape),
            in_specs=[smem, vmem, vmem, vmem, vmem] + [anywhere] * 6,
            out_specs=(anywhere, anywhere, anywhere),
            scratch_shapes=[
                pltpu.VMEM((ROWS, D), bf16), pltpu.VMEM((ROWS, D), bf16), pltpu.VMEM((RING, D, TILE), bf16),
                pltpu.VMEM((HEADS + 2 * KV, ROWS, HEAD), f32),
                pltpu.VMEM((REQ, NBLK, KV, BLK, HEAD), bf16), pltpu.VMEM((REQ, NBLK, KV, BLK, HEAD), bf16),
                pltpu.VMEM((REQ, TREE, EXT), f32),
                dma, dma((RING,)), dma((REQ,)), dma((REQ,)), dma((REQ,)), dma((REQ,)), dma((REQ,)),
            ],
            compiler_params=pltpu.CompilerParams(vmem_limit_bytes=62 * 1024 * 1024),
            cost_estimate=pl.CostEstimate(flops=20_000_000_000, bytes_accessed=72_000_000, transcendentals=5_000_000),
            name='attend',
        )(ctx_len, attn_gain.reshape(1, D), cos_tab, sin_tab, tree_mask, flat, w_query, w_key, w_value, cache_k, cache_v)
        pieces = pltpu.VMEM((NP, MINE, W), f32)
        out = pl.pallas_call(
            tail_kernel,
            out_shape=jax.ShapeDtypeStruct((ROWS, D), bf16),
            in_specs=[anywhere] * 3,
            out_specs=vmem,
            scratch_shapes=[
                pltpu.VMEM((REQ, TREE, EXT), f32), pltpu.VMEM((6, TREE, EXT), f32), pltpu.VMEM((3, TREE, EXT), f32),
                pltpu.VMEM((3, TREE, EXT), f32), pltpu.VMEM((3, TREE, EXT), f32), pltpu.VMEM((6, TREE, WIDE), f32),
                pltpu.VMEM((MINE, WIDE), bf16), pltpu.VMEM((NP, WIDE, W), bf16), pltpu.VMEM((MINE, HALF), bf16),
                pieces, pieces, pieces, pieces, pieces, pieces, pieces,
                dma((REQ,)), dma((NP,)), dma, dma((6,)), dma((6,)), dma((3,)), dma((3,)), dma((3,)), dma((3,)),
            ] + [dma((NP,)) for _ in range(12)],
            compiler_params=pltpu.CompilerParams(vmem_limit_bytes=62 * 1024 * 1024, collective_id=0, has_side_effects=True),
            cost_estimate=pl.CostEstimate(flops=2_500_000_000, bytes_accessed=30_000_000, transcendentals=100_000),
            name='tail',
        )(partial_out, w_out, flat)
        return out.reshape(REQ, TREE, D), new_k, new_v

    return jax.shard_map(local_step, mesh=mesh, in_specs=(row_spec, P(), P(None, 'tp'), P(None, 'tp'), P(None, 'tp'), P('tp', None), cache_spec, cache_spec, row_spec, row_spec, row_spec), out_specs=(row_spec, cache_spec, cache_spec), check_vma=False)
```

time: 599 us -> 145 us (0.24)
  waiting for transfers between devices: 276 us -> 0 us
  local copies, waits for them, and re-layouts: 165 us -> 6.46 us
  Pallas kernels: 0 us -> 135 us
  matrix products: 73 us -> 0 us
  blocking collectives: 33.4 us -> 0 us
  other arithmetic: 34.6 us -> 2.17 us
  between operations: 14.3 us -> 0.66 us
    psum x2 -> x0, waiting for transfers between devices: 276 us -> none  [the longest x1 233 us: local_step(): proj_sum = lax.psum(proj_part.astype(jnp.float32), 'tp')]
    pallas_call x0 -> x2, Pallas kernels: none -> 135 us  [the longest x1 94.9 us: local_step(): pl.pallas_call(tail_kernel, out_shape=jax.ShapeDtypeStruct((ROWS, D), bf1...]
    scatter x2 -> x0, local copies, waits for them, and re-layouts: 73.8 us -> none  [the longest x1 37.1 us: local_step(): keys.at[req_ids, local_blk, :, slot_ids % blk_len, :]]
    dot_general x8 -> x0, matrix products: 73 us -> none  [the longest x1 18.1 us: local_step(): jnp.einsum('rtf,fe->rte', attn_out, w_out, preferred_element_type=jnp.flo...]
    dot_general x2 -> x0, local copies, waits for them, and re-layouts: 46.8 us -> none  [the longest x1 40.4 us: local_step(): jnp.dot(flat_rows, w_query, preferred_element_type=jnp.float32)]
    unnamed x26 -> x1, local copies, waits for them, and re-layouts: 39.5 us -> 5.03 us
    pmax x1 -> x0, blocking collectives: 16.8 us -> none  [local_step(): glob_max = lax.pmax(row_max, 'cp')]
    psum x1 -> x0, blocking collectives: 16.6 us -> none  [local_step(): glob_sum = lax.psum(row_sum * factor, 'cp')]
  transfers between devices with their start and end apart: 2 -> 0, of which waited for: 2 -> 0; matrix products, arithmetic and copies ran while one was open for 15% -> 0% of each run, Pallas kernels for 0% -> 0%
where the time goes in v1:
time: 145 us
  Pallas kernels  135 us (93%)
  local copies, waits for them, and re-layouts  6.46 us (4%)
  other arithmetic  2.17 us (1%)
    pallas_call x1, Pallas kernels, local_step(): pl.pallas_call(tail_kernel, out_shape=jax.ShapeDtypeStruct((ROWS, D), bf1...  94.9 us
    pallas_call x1, Pallas kernels, local_step(): pl.pallas_call(attend_kernel, out_shape=(jax.ShapeDtypeStruct((REQ, TREE,...  40.5 us
    unnamed x1, local copies, waits for them, and re-layouts  5.03 us

profile of v1, /device:TPU:0, one launch (start us, length us, event | category | flops | bytes accessed | tf_op | source)
XLA Modules:
  0.0 144.7 jit_solution(8874169706350367509)
XLA Ops:
  0.7 0.7 convert_element_type.3
  1.4 0.1 mul.31
  1.4 1.3 reshape.39.gain_ref
  2.8 0.6 fusion
  3.4 0.9 pad_maximum_fusion
  4.2 40.5 %attend.1 = (f32[12,24,2176]{2,1,0:T(8,128)}, bf16[12,4,1,2,256,128]{5,4,3,2,1,0:T(8,128)(2,1)}, bf16[12,4,1,2,256,128]{5,4,3,2,1,0:T(8,128)(2,1)}) custom-call(s32[12]{0:T(128)} %ctx_ref.1, bf16[1,8192]{1,0:T(2,128)(2,1)} %reshape.39.gain_ref, f32[288,128]{1,0:T(8,128)} %get-tuple-element.12.cos_ref, f32[288,128]{1,0:T(8,128)} %get-tuple-element.13.sin_ref, ...), custom_call_target="tpu_custom_call" | custom-call | flops 20000000000 | bytes 72000000 | tf_op jit(solution)/shard_map/attend/pallas_call | solution.py:430
  44.8 94.9 %tail.1 = bf16[288,8192]{1,0:T(8,128)(2,1)} custom-call(f32[12,24,2176]{2,1,0:T(8,128)} %get-tuple-element.6.o_hbm, bf16[2048,8192]{1,0:T(8,128)(2,1)} %w_hbm.1, bf16[288,8192]{1,0:T(8,128)(2,1)} %bitcast.4), custom_call_target="tpu_custom_call" | custom-call | flops 2500000000 | bytes 30000000 | tf_op jit(solution)/shard_map/tail/pallas_call | solution.py:447
  139.7 5.0 %copy.15 = bf16[12,24,8192]{2,1,0:T(8,128)(2,1)} copy(bf16[12,24,8192]{2,1,0:T(8,128)(2,1)} %bitcast.2) | data formatting | bytes 9437184
  (1 shorter events, 0.0 us)

commit v2 on v1

v2 whole, which is shorter than its diff:
```python
import math
import jax
import jax.numpy as jnp
from jax import lax
from jax.experimental import pallas as pl
from jax.experimental.pallas import tpu as pltpu
from jax.sharding import PartitionSpec as P

ROPE_THETA = 500000.0
NORM_EPS = 1e-5
MASKED = -1e30
LOG2E = 1.4426950408889634
MESH = pl.DeviceIdType.MESH

REQ = 12
TREE = 24
ROWS = REQ * TREE
D = 8192
HEAD = 128
KV = 2
GROUP = 8
HEADS = KV * GROUP
NBLK = 4
BLK = 256
CP = 4
WIDE = HEADS * HEAD
EXT = WIDE + HEAD
TILE = 256
NTILE = (HEADS + 2 * KV) * HEAD // TILE
RING = 4
HALF = D // 2
NP = 16
W = HALF // NP
WAVES = 3
WAVE_ROWS = CP * TREE
PART_ROWS = WAVE_ROWS // 2
PIECES = WAVES * NP
AHEAD = 8


def rope_tables(positions):
    freq_idx = jnp.arange(HEAD // 2, dtype=jnp.float32)
    inv_freq = 1.0 / (ROPE_THETA ** (2.0 * freq_idx / HEAD))
    wavelen = 2.0 * math.pi / inv_freq
    smooth = (8192.0 / wavelen - 1.0) / 3.0
    blended = (1.0 - smooth) * inv_freq / 8.0 + smooth * inv_freq
    inv_freq = jnp.where(wavelen < 2048.0, inv_freq, jnp.where(wavelen > 8192.0, inv_freq / 8.0, blended))
    angle = positions.astype(jnp.float32)[..., None] * inv_freq
    return jnp.cos(angle).reshape(ROWS, HEAD // 2), jnp.sin(angle).reshape(ROWS, HEAD // 2)


def attend_kernel(ctx_ref, gain_ref, cos_ref, sin_ref, mask_ref, x_hbm, wq_hbm, wk_hbm, wv_hbm, ck_hbm, cv_hbm,
                  o_ref, nk_hbm, nv_hbm,
                  x_ref, h_ref, turn, wbuf, qkv, kbuf, vbuf, xsem, wsem, ksem, vsem, nksem, nvsem):
    cp_rank = lax.axis_index('cp')
    nq = HEADS * HEAD // TILE

    x_copy = pltpu.make_async_copy(x_hbm, x_ref, xsem)
    x_copy.start()

    def start_weight(i):
        slot = lax.rem(i, RING)

        @pl.when(i < nq)
        def _():
            cols = pl.ds(pl.multiple_of(i * TILE, TILE), TILE)
            pltpu.make_async_copy(wq_hbm.at[:, cols], wbuf.at[slot], wsem.at[slot]).start()

        @pl.when(i == nq)
        def _():
            pltpu.make_async_copy(wk_hbm, wbuf.at[slot], wsem.at[slot]).start()

        @pl.when(i == nq + 1)
        def _():
            pltpu.make_async_copy(wv_hbm, wbuf.at[slot], wsem.at[slot]).start()

    def start_cache(r):
        pltpu.make_async_copy(ck_hbm.at[r, :, 0], kbuf.at[r], ksem.at[r]).start()
        pltpu.make_async_copy(cv_hbm.at[r, :, 0], vbuf.at[r], vsem.at[r]).start()

    for i in range(RING):
        start_weight(jnp.int32(i))
    turn[0] = jnp.concatenate([cos_ref[...], cos_ref[...]], axis=-1)
    turn[1] = jnp.concatenate([-sin_ref[...], sin_ref[...]], axis=-1)
    x_copy.wait()

    def norm_step(i, carry):
        rows = pl.ds(pl.multiple_of(i * 16, 16), 16)
        squares = [jnp.zeros((16, HEAD), jnp.float32) for _ in range(2)]
        for k in range(D // HEAD):
            wide = x_ref[rows, k * HEAD:(k + 1) * HEAD].astype(jnp.float32)
            squares[k % 2] = squares[k % 2] + wide * wide
        inv = lax.rsqrt(jnp.sum(squares[0] + squares[1], axis=-1, keepdims=True) * (1.0 / D) + NORM_EPS)
        for k in range(D // HEAD):
            cols = slice(k * HEAD, (k + 1) * HEAD)
            wide = x_ref[rows, cols].astype(jnp.float32)
            h_ref[rows, cols] = (wide * inv * gain_ref[cols].astype(jnp.float32).reshape(1, HEAD)).astype(jnp.bfloat16)
        return carry

    lax.fori_loop(0, ROWS // 16, norm_step, 0)

    def proj_step(i, carry):
        slot = lax.rem(i, RING)
        pltpu.make_async_copy(wk_hbm, wbuf.at[slot], wsem.at[slot]).wait()
        acc = jnp.dot(h_ref[...], wbuf[slot], preferred_element_type=jnp.float32)
        for hh in range(TILE // HEAD):
            part = acc[:, hh * HEAD:(hh + 1) * HEAD]
            turned = pltpu.roll(part, HEAD // 2, 1)
            cos_tab = jnp.where(i < NTILE - 1, turn[0], 1.0)
            sin_tab = jnp.where(i < NTILE - 1, turn[1], 0.0)
            qkv[(TILE // HEAD) * i + hh] = part * cos_tab + turned * sin_tab

        @pl.when(i + RING < NTILE)
        def _():
            start_weight(i + RING)

        @pl.when(i + RING >= NTILE)
        def _():
            start_cache(i + RING - NTILE)
        return carry

    lax.fori_loop(0, NTILE, proj_step, 0)

    def attend_step(r, carry):
        @pl.when(r + RING < REQ)
        def _():
            start_cache(r + RING)

        pltpu.make_async_copy(ck_hbm.at[r, :, 0], kbuf.at[r], ksem.at[r]).wait()
        pltpu.make_async_copy(cv_hbm.at[r, :, 0], vbuf.at[r], vsem.at[r]).wait()
        ctx = ctx_ref[r]
        rows = pl.ds(pl.multiple_of(r * TREE, 8), TREE)
        first = ctx // BLK
        last = (ctx + TREE - 1) // BLK

        def insert(block):
            j = block // CP
            slot_of = lax.broadcasted_iota(jnp.int32, (BLK, TREE), 0) + (block * BLK - ctx)
            pick = (slot_of == lax.broadcasted_iota(jnp.int32, (BLK, TREE), 1)).astype(jnp.bfloat16)
            wide_slot = lax.broadcasted_iota(jnp.int32, (BLK, HEAD), 0) + (block * BLK - ctx)
            inside = (wide_slot >= 0) & (wide_slot < TREE)
            for hd in range(KV):
                for buf, base in ((kbuf, HEADS), (vbuf, HEADS + KV)):
                    new = qkv[base + hd, rows, :].astype(jnp.bfloat16)
                    placed = jnp.dot(pick, new, preferred_element_type=jnp.float32)
                    old = buf[r, j, hd].astype(jnp.float32)
                    buf[r, j, hd] = jnp.where(inside, placed, old).astype(jnp.bfloat16)

        @pl.when(lax.rem(first, CP) == cp_rank)
        def _():
            insert(first)

        @pl.when((lax.rem(last, CP) == cp_rank) & (last != first))
        def _():
            insert(last)

        pltpu.make_async_copy(kbuf.at[r], nk_hbm.at[r, :, 0], nksem.at[r]).start()
        pltpu.make_async_copy(vbuf.at[r], nv_hbm.at[r, :, 0], nvsem.at[r]).start()

        lane = lax.broadcasted_iota(jnp.int32, (TREE, NBLK * BLK), 1)
        pos = (lane // BLK * CP + cp_rank) * BLK + lane % BLK - ctx
        onehot = (pos == lax.broadcasted_iota(jnp.int32, (TREE, NBLK * BLK), 0)).astype(jnp.bfloat16)
        allowed = jnp.dot(mask_ref[r].astype(jnp.float32).astype(jnp.bfloat16), onehot, preferred_element_type=jnp.float32)
        bias = jnp.where((pos < 0) | (allowed > 0.5), 0.0, MASKED)

        stats = jnp.zeros((TREE, HEAD), jnp.float32)
        stat_lane = lax.broadcasted_iota(jnp.int32, (TREE, HEAD), 1)
        for hd in range(KV):
            query = qkv[hd * GROUP:(hd + 1) * GROUP, rows, :].reshape(GROUP * TREE, HEAD).astype(jnp.bfloat16)
            keys = kbuf[r, :, hd].reshape(NBLK * BLK, HEAD)
            vals = vbuf[r, :, hd].reshape(NBLK * BLK, HEAD)
            score = lax.dot_general(query, keys, (((1,), (1,)), ((), ())), preferred_element_type=jnp.float32)
            score = score.reshape(GROUP, TREE, NBLK * BLK) * (HEAD ** -0.5 * LOG2E) + bias[None]
            top = jnp.max(score, axis=-1, keepdims=True)
            prob = jnp.exp2(score - top)
            total = jnp.sum(prob, axis=-1, keepdims=True)
            mixed = jnp.dot(prob.reshape(GROUP * TREE, NBLK * BLK).astype(jnp.bfloat16), vals, preferred_element_type=jnp.float32)
            for g in range(GROUP):
                head = hd * GROUP + g
                o_ref[r, :, head * HEAD:(head + 1) * HEAD] = mixed[g * TREE:(g + 1) * TREE]
                stats = jnp.where(stat_lane == head, top[g], stats)
                stats = jnp.where(stat_lane == HEADS + head, total[g], stats)
        o_ref[r, :, WIDE:] = stats
        return carry

    lax.fori_loop(0, REQ, attend_step, 0)

    def drain(r, carry):
        pltpu.make_async_copy(kbuf.at[r], nk_hbm.at[r, :, 0], nksem.at[r]).wait()
        pltpu.make_async_copy(vbuf.at[r], nv_hbm.at[r, :, 0], nvsem.at[r]).wait()
        return carry

    lax.fori_loop(0, REQ, drain, 0)


def merge(a, b):
    ta, tb = a[:, WIDE:], b[:, WIDE:]
    top = jnp.maximum(ta, tb)
    fa, fb = jnp.exp2(ta - top), jnp.exp2(tb - top)
    total = ta * pltpu.roll(fa, HEADS, 1) + tb * pltpu.roll(fb, HEADS, 1)
    lane = lax.broadcasted_iota(jnp.int32, (TREE, HEAD), 1)
    return fa, fb, total, jnp.where(lane < HEADS, top, total)


def tail_kernel(own, w_hbm, x_hbm, y_ref,
                pin, yrecv, heads, hbf, wbuf, xbuf,
                part, in_end, in_mid, fin, fin_y, fin_c, fin_cy,
                wsem, xsem, s_p, r_p, s_y, r_y, s_a, r_a,
                s_e, r_e, s_m, r_m, s_f, r_f, s_yf, r_yf, s_cf, r_cf, s_cy, r_cy):
    cp_rank = lax.axis_index('cp')
    z = lax.axis_index('tp')
    yy = cp_rank // 2
    core = cp_rank % 2
    other_core = 1 - core
    other_y = 1 - yy
    mid = (z + 1) // 2 % 2
    partner = {'cp': yy * 2 + other_core}
    across = {'cp': other_y * 2 + core}
    pair = {'tp': z + 1 - 2 * (z % 2)}
    middle = {'tp': 3 - z}

    def remote(src, dst, send, recv, peer):
        return pltpu.make_async_remote_copy(src_ref=src, dst_ref=dst, send_sem=send, recv_sem=recv, device_id=peer, device_id_type=MESH)

    barrier = pltpu.get_barrier_semaphore()
    for peer in (partner, across, pair):
        pl.semaphore_signal(barrier, inc=1, device_id=peer, device_id_type=MESH)

    @pl.when(mid == 1)
    def _():
        pl.semaphore_signal(barrier, inc=1, device_id=middle, device_id_type=MESH)

    def weight_copy(j):
        cols = pl.ds(pl.multiple_of(core * HALF + j * W, W), W)
        return pltpu.make_async_copy(w_hbm.at[:, cols], wbuf.at[j], wsem.at[j])

    def start_weight(j, carry):
        weight_copy(j).start()
        return carry

    lax.fori_loop(0, NP, start_weight, 0)
    x_copies = [pltpu.make_async_copy(
        x_hbm.at[pl.ds(pl.multiple_of(w * WAVE_ROWS + yy * PART_ROWS, 16), PART_ROWS), pl.ds(pl.multiple_of(core * HALF, HALF), HALF)],
        xbuf.at[w], xsem.at[w]) for w in range(WAVES)]
    for copy in x_copies:
        copy.start()

    @pl.when(mid == 1)
    def _():
        pl.semaphore_wait(barrier, 4)

    @pl.when(mid == 0)
    def _():
        pl.semaphore_wait(barrier, 3)

    def chip_copy(w, side):
        chip = yy if side else other_y
        return remote(own.at[4 * w + 2 * chip + other_core], pin.at[w, side], s_p.at[w, side], r_p.at[w, side], partner)

    for w in range(WAVES):
        for side in (0, 1):
            chip_copy(w, side).start()

    def y_copy(w):
        return remote(pin.at[w, 0], yrecv.at[w], s_y.at[w], r_y.at[w], across)

    def blend(a, b):
        fa, fb, total, stats = merge(a, b)
        for h in range(HEADS):
            cols = slice(h * HEAD, (h + 1) * HEAD)
            b[:, cols] = a[:, cols] * fa[:, h:h + 1] + b[:, cols] * fb[:, h:h + 1]
        b[:, WIDE:] = stats

    def head_copy(w, owner):
        return remote(heads.at[w, owner], heads.at[w, owner], s_a.at[w], r_a.at[w], partner)

    def finish_start(w):
        y_copy(w).wait_recv()
        a, b, out = pin.at[w, 1], yrecv.at[w], heads.at[w, core]
        fa, fb, total, stats = merge(a, b)
        inv = 1.0 / total
        for h in range(HEADS):
            cols = slice(h * HEAD, (h + 1) * HEAD)
            mixed = a[:, cols] * fa[:, h:h + 1] + b[:, cols] * fb[:, h:h + 1]
            out[:, cols] = mixed * inv[:, HEADS + h:HEADS + h + 1]
        head_copy(w, core).start()

    def finish_end(w):
        head_copy(w, other_core).wait_recv()
        hbf[...] = heads[w].reshape(PART_ROWS, WIDE).astype(jnp.bfloat16)

    for w in range(WAVES):
        chip_copy(w, 0).wait_recv()
        blend(own.at[4 * w + 2 * other_y + core], pin.at[w, 0])
        y_copy(w).start()
    for w in range(WAVES):
        chip_copy(w, 1).wait_recv()
        blend(own.at[4 * w + 2 * yy + core], pin.at[w, 1])
    for copy in x_copies:
        copy.wait()
    finish_start(0)
    finish_end(0)

    def end_copy(p):
        return remote(part.at[p], in_end.at[p], s_e.at[p], r_e.at[p], pair)

    def mid_copy(p):
        return remote(part.at[p], in_mid.at[p], s_m.at[p], r_m.at[p], middle)

    def fin_copy(p):
        return remote(fin.at[p], fin.at[p], s_f.at[p], r_f.at[p], pair)

    def across_copy(p):
        return remote(fin.at[p], fin_y.at[p], s_yf.at[p], r_yf.at[p], across)

    def core_copy(p):
        return remote(fin.at[p], fin_c.at[p], s_cf.at[p], r_cf.at[p], partner)

    def core_y_copy(p):
        return remote(fin_y.at[p], fin_cy.at[p], s_cy.at[p], r_cy.at[p], partner)

    def project(p):
        j = p % NP

        @pl.when(p < NP)
        def _():
            weight_copy(j).wait()

        prod = jnp.dot(hbf[...], wbuf[j], preferred_element_type=jnp.float32)
        part[p] = prod.astype(jnp.bfloat16).astype(jnp.float32)

        @pl.when(mid == 0)
        def _():
            end_copy(p).start()

    def emit(buf, p, chip, half):
        rows = pl.ds(pl.multiple_of(p // NP * WAVE_ROWS + chip * PART_ROWS, 16), PART_ROWS)
        cols = pl.ds(pl.multiple_of(half * HALF + p % NP * W, W), W)
        y_ref[rows, cols] = buf[p].astype(jnp.bfloat16)

    def take_end(p):
        end_copy(p).wait_recv()
        part[p] = part[p] + in_end[p]
        mid_copy(p).start()

    def take_mid(p):
        mid_copy(p).wait_recv()
        xcols = pl.ds(pl.multiple_of(p % NP * W, W), W)
        fin[p] = (part[p] + in_mid[p]) + xbuf[p // NP, :, xcols].astype(jnp.float32)
        fin_copy(p).start()
        across_copy(p).start()
        core_copy(p).start()
        emit(fin, p, yy, core)

    def take_fin(p):
        fin_copy(p).wait_recv()
        across_copy(p).start()
        core_copy(p).start()
        emit(fin, p, yy, core)

    def take_core(p):
        core_copy(p).wait_recv()
        emit(fin_c, p, yy, other_core)

    def take_across(p):
        across_copy(p).wait_recv()
        core_y_copy(p).start()
        emit(fin_y, p, other_y, core)

    def take_core_y(p):
        core_y_copy(p).wait_recv()
        emit(fin_cy, p, other_y, other_core)

    def ahead_step(p, carry):
        project(p)
        return carry

    lax.fori_loop(0, AHEAD, ahead_step, 0)
    lag = lambda at_mid, at_end: jnp.where(mid == 1, at_mid, at_end)
    lag_core, lag_across, lag_core_y = lag(6, 9), lag(8, 11), lag(10, 13)

    def step(s, carry):
        for w in range(1, WAVES):
            @pl.when(s == w * NP - AHEAD - 4)
            def _():
                finish_start(w)

            @pl.when(s == w * NP - AHEAD)
            def _():
                finish_end(w)

        @pl.when(s + AHEAD < PIECES)
        def _():
            project(s + AHEAD)

        @pl.when((mid == 1) & (s < PIECES))
        def _():
            take_end(s)

        @pl.when((mid == 1) & (s >= 4) & (s < PIECES + 4))
        def _():
            take_mid(s - 4)

        @pl.when((mid == 0) & (s >= 7) & (s < PIECES + 7))
        def _():
            take_fin(s - 7)

        for this_lag, body in ((lag_core, take_core), (lag_across, take_across), (lag_core_y, take_core_y)):
            p = s - this_lag

            @pl.when((p >= 0) & (p < PIECES))
            def _():
                body(p)
        return carry

    lax.fori_loop(0, PIECES + 13, step, 0)

    for w in range(WAVES):
        for side in (0, 1):
            chip_copy(w, side).wait_send()
        y_copy(w).wait_send()
        head_copy(w, core).wait_send()

    def sent(p, carry):
        across_copy(p).wait_send()
        core_copy(p).wait_send()
        core_y_copy(p).wait_send()

        @pl.when(mid == 1)
        def _():
            mid_copy(p).wait_send()
            fin_copy(p).wait_send()

        @pl.when(mid == 0)
        def _():
            end_copy(p).wait_send()
        return carry

    lax.fori_loop(0, PIECES, sent, 0)


def solution(mesh):
    cache_spec = P('dp', None, 'cp', 'tp')
    row_spec = P('dp')
    anywhere = pl.BlockSpec(memory_space=pl.ANY)
    vmem = pl.BlockSpec(memory_space=pltpu.VMEM)
    smem = pl.BlockSpec(memory_space=pltpu.SMEM)
    dma = pltpu.SemaphoreType.DMA
    f32, bf16 = jnp.float32, jnp.bfloat16

    def local_step(hidden, attn_gain, w_query, w_key, w_value, w_out, cache_k, cache_v, ctx_len, positions, tree_mask):
        cos_tab, sin_tab = rope_tables(positions)
        flat = hidden.reshape(ROWS, D)
        cache_shape = jax.ShapeDtypeStruct(cache_k.shape, bf16)
        partial_out, new_k, new_v = pl.pallas_call(
            attend_kernel,
            out_shape=(pltpu.VMEM((REQ, TREE, EXT), f32), cache_shape, cache_shape),
            in_specs=[smem, vmem, vmem, vmem, vmem] + [anywhere] * 6,
            out_specs=(vmem, anywhere, anywhere),
            scratch_shapes=[
                pltpu.VMEM((ROWS, D), bf16), pltpu.VMEM((ROWS, D), bf16), pltpu.VMEM((2, ROWS, HEAD), f32), pltpu.VMEM((RING, D, TILE), bf16),
                pltpu.VMEM((HEADS + 2 * KV, ROWS, HEAD), f32),
                pltpu.VMEM((REQ, NBLK, KV, BLK, HEAD), bf16), pltpu.VMEM((REQ, NBLK, KV, BLK, HEAD), bf16),
                dma, dma((RING,)), dma((REQ,)), dma((REQ,)), dma((REQ,)), dma((REQ,)),
            ],
            compiler_params=pltpu.CompilerParams(vmem_limit_bytes=56 * 1024 * 1024),
            cost_estimate=pl.CostEstimate(flops=20_000_000_000, bytes_accessed=72_000_000, transcendentals=5_000_000),
            name='attend',
        )(ctx_len, attn_gain, pltpu.with_memory_space_constraint(cos_tab, pltpu.VMEM), pltpu.with_memory_space_constraint(sin_tab, pltpu.VMEM), tree_mask, flat, w_query, w_key, w_value, cache_k, cache_v)
        pieces = pltpu.VMEM((PIECES, PART_ROWS, W), f32)
        out = pl.pallas_call(
            tail_kernel,
            out_shape=pltpu.VMEM((ROWS, D), bf16),
            in_specs=[vmem, anywhere, anywhere],
            out_specs=vmem,
            scratch_shapes=[
                pltpu.VMEM((WAVES, 2, TREE, EXT), f32), pltpu.VMEM((WAVES, TREE, EXT), f32), pltpu.VMEM((WAVES, 2, TREE, WIDE), f32),
                pltpu.VMEM((PART_ROWS, WIDE), bf16), pltpu.VMEM((NP, WIDE, W), bf16), pltpu.VMEM((WAVES, PART_ROWS, HALF), bf16),
                pieces, pieces, pieces, pieces, pieces, pieces, pieces,
                dma((NP,)), dma((WAVES,)), dma((WAVES, 2)), dma((WAVES, 2)), dma((WAVES,)), dma((WAVES,)), dma((WAVES,)), dma((WAVES,)),
            ] + [dma((PIECES,)) for _ in range(12)],
            compiler_params=pltpu.CompilerParams(vmem_limit_bytes=48 * 1024 * 1024, collective_id=0, has_side_effects=True),
            cost_estimate=pl.CostEstimate(flops=2_500_000_000, bytes_accessed=30_000_000, transcendentals=100_000),
            name='tail',
        )(pltpu.with_memory_space_constraint(partial_out, pltpu.VMEM), w_out, flat)
        return out.reshape(REQ, TREE, D), new_k, new_v

    return jax.shard_map(local_step, mesh=mesh, in_specs=(row_spec, P(), P(None, 'tp'), P(None, 'tp'), P(None, 'tp'), P('tp', None), cache_spec, cache_spec, row_spec, row_spec, row_spec), out_specs=(row_spec, cache_spec, cache_spec), check_vma=False)
```

time: 145 us -> 123 us (0.85)
  Pallas kernels: 135 us -> 119 us
  local copies, waits for them, and re-layouts: 6.46 us -> 2.27 us
    pallas_call x2, Pallas kernels: 135 us -> 119 us  [the longest x1 83.2 us: local_step(): pl.pallas_call(tail_kernel, out_shape=pltpu.VMEM((ROWS, D), bf16), in_spe...]
    unnamed x1, local copies, waits for them, and re-layouts: 5.03 us -> 2.19 us
where the time goes in v2:
time: 123 us
  Pallas kernels  119 us (97%)
  local copies, waits for them, and re-layouts  2.27 us (2%)
  other arithmetic  1.31 us (1%)
    pallas_call x1, Pallas kernels, local_step(): pl.pallas_call(tail_kernel, out_shape=pltpu.VMEM((ROWS, D), bf16), in_spe...  83.2 us
    pallas_call x1, Pallas kernels, local_step(): pl.pallas_call(attend_kernel, out_shape=(pltpu.VMEM((REQ, TREE, EXT), f32...  35.4 us

profile of v2, /device:TPU:0, one launch (start us, length us, event | category | flops | bytes accessed | tf_op | source)
XLA Modules:
  0.0 122.9 jit_solution(973023907703589440)
XLA Ops:
  0.7 0.7 convert_element_type.3
  1.4 0.1 mul.33
  1.4 0.6 multiply_sine_fusion
  2.0 35.4 %attend.1 = (f32[12,24,2176]{2,1,0:T(8,128)S(1)}, bf16[12,4,1,2,256,128]{5,4,3,2,1,0:T(8,128)(2,1)}, bf16[12,4,1,2,256,128]{5,4,3,2,1,0:T(8,128)(2,1)}) custom-call(s32[12]{0:T(128)} %ctx_ref.1, bf16[8192]{0:T(1024)(128)(2,1)} %gain_ref.1, f32[288,64]{1,0:T(8,128)S(1)} %get-tuple-element.10.cos_ref, f32[288,64]{1,0:T(8,128)S(1)} %get-tuple-element.9.sin_ref, ...), custom_call_target="tpu_custom_call" | custom-call | flops 20000000000 | bytes 72000000 | tf_op jit(solution)/shard_map/attend/pallas_call | solution.py:455
  37.5 83.2 %tail.1 = bf16[288,8192]{1,0:T(8,128)(2,1)S(1)} custom-call(f32[12,24,2176]{2,1,0:T(8,128)S(1)} %get-tuple-element.6.own, bf16[2048,8192]{1,0:T(8,128)(2,1)} %w_hbm.1, bf16[288,8192]{1,0:T(8,128)(2,1)} %bitcast.4), custom_call_target="tpu_custom_call" | custom-call | flops 2500000000 | bytes 30000000 | tf_op jit(solution)/shard_map/tail/pallas_call | solution.py:471
  120.7 2.2 %copy.15 = bf16[12,24,8192]{2,1,0:T(8,128)(2,1)} copy(bf16[12,24,8192]{2,1,0:T(8,128)(2,1)S(1)} %bitcast.2) | data formatting | bytes 9437184
  (1 shorter events, 0.0 us)

commit v3 on v2

--- a/solution.py
+++ b/solution.py
@@ -9,6 +9,7 @@
 ROPE_THETA = 500000.0
 NORM_EPS = 1e-5
 MASKED = -1e30
+UNROLL = 2
 LOG2E = 1.4426950408889634
 MESH = pl.DeviceIdType.MESH
 
@@ -28,6 +29,10 @@
 TILE = 256
 NTILE = (HEADS + 2 * KV) * HEAD // TILE
 RING = 4
+XCHUNKS = 3
+CACHE_AHEAD = 8
+EARLY = 8
+LATE = REQ - EARLY
 HALF = D // 2
 NP = 16
 W = HALF // NP
@@ -50,13 +55,16 @@
 
 
 def attend_kernel(ctx_ref, gain_ref, cos_ref, sin_ref, mask_ref, x_hbm, wq_hbm, wk_hbm, wv_hbm, ck_hbm, cv_hbm,
-                  o_ref, nk_hbm, nv_hbm,
-                  x_ref, h_ref, turn, wbuf, qkv, kbuf, vbuf, xsem, wsem, ksem, vsem, nksem, nvsem):
+                  o_ref, qkv, nk_hbm, nv_hbm,
+                  x_ref, h_ref, turn, wbuf, kbuf, vbuf, xsem, wsem, ksem, vsem, nksem, nvsem):
     cp_rank = lax.axis_index('cp')
     nq = HEADS * HEAD // TILE
 
-    x_copy = pltpu.make_async_copy(x_hbm, x_ref, xsem)
-    x_copy.start()
+    x_copies = []
+    for k in range(XCHUNKS):
+        rows = pl.ds(k * (ROWS // XCHUNKS), ROWS // XCHUNKS)
+        x_copies.append(pltpu.make_async_copy(x_hbm.at[rows, :], x_ref.at[rows, :], xsem.at[k]))
+        x_copies[k].start()
 
     def start_weight(i):
         slot = lax.rem(i, RING)
@@ -78,12 +86,8 @@
         pltpu.make_async_copy(ck_hbm.at[r, :, 0], kbuf.at[r], ksem.at[r]).start()
         pltpu.make_async_copy(cv_hbm.at[r, :, 0], vbuf.at[r], vsem.at[r]).start()
 
-    for i in range(RING):
-        start_weight(jnp.int32(i))
     turn[0] = jnp.concatenate([cos_ref[...], cos_ref[...]], axis=-1)
     turn[1] = jnp.concatenate([-sin_ref[...], sin_ref[...]], axis=-1)
-    x_copy.wait()
-
     def norm_step(i, carry):
         rows = pl.ds(pl.multiple_of(i * 16, 16), 16)
         squares = [jnp.zeros((16, HEAD), jnp.float32) for _ in range(2)]
@@ -97,17 +101,23 @@
             h_ref[rows, cols] = (wide * inv * gain_ref[cols].astype(jnp.float32).reshape(1, HEAD)).astype(jnp.bfloat16)
         return carry
 
-    lax.fori_loop(0, ROWS // 16, norm_step, 0)
+    for k in range(XCHUNKS):
+        x_copies[k].wait()
+        if k == 0:
+            for i in range(RING):
+                start_weight(jnp.int32(i))
+        lax.fori_loop(k * (ROWS // 16 // XCHUNKS), (k + 1) * (ROWS // 16 // XCHUNKS), norm_step, 0)
 
     def proj_step(i, carry):
         slot = lax.rem(i, RING)
-        pltpu.make_async_copy(wk_hbm, wbuf.at[slot], wsem.at[slot]).wait()
+        pltpu.make_async_copy(wq_hbm.at[:, :TILE], wbuf.at[slot], wsem.at[slot]).wait()
         acc = jnp.dot(h_ref[...], wbuf[slot], preferred_element_type=jnp.float32)
         for hh in range(TILE // HEAD):
             part = acc[:, hh * HEAD:(hh + 1) * HEAD]
             turned = pltpu.roll(part, HEAD // 2, 1)
-            cos_tab = jnp.where(i < NTILE - 1, turn[0], 1.0)
-            sin_tab = jnp.where(i < NTILE - 1, turn[1], 0.0)
+            cos_tab, sin_tab = turn[0], turn[1]
+            cos_tab = jnp.where(i < NTILE - 1, cos_tab, 1.0)
+            sin_tab = jnp.where(i < NTILE - 1, sin_tab, 0.0)
             qkv[(TILE // HEAD) * i + hh] = part * cos_tab + turned * sin_tab
 
         @pl.when(i + RING < NTILE)
@@ -116,15 +126,16 @@
 
         @pl.when(i + RING >= NTILE)
         def _():
-            start_cache(i + RING - NTILE)
+            for k in range(CACHE_AHEAD // RING):
+                start_cache((i + RING - NTILE) * (CACHE_AHEAD // RING) + k)
         return carry
 
     lax.fori_loop(0, NTILE, proj_step, 0)
 
-    def attend_step(r, carry):
-        @pl.when(r + RING < REQ)
-        def _():
-            start_cache(r + RING)
+    def prepare(r):
+        @pl.when(r + CACHE_AHEAD < REQ)
+        def _():
+            start_cache(r + CACHE_AHEAD)
 
         pltpu.make_async_copy(ck_hbm.at[r, :, 0], kbuf.at[r], ksem.at[r]).wait()
         pltpu.make_async_copy(cv_hbm.at[r, :, 0], vbuf.at[r], vsem.at[r]).wait()
@@ -157,6 +168,10 @@
         pltpu.make_async_copy(kbuf.at[r], nk_hbm.at[r, :, 0], nksem.at[r]).start()
         pltpu.make_async_copy(vbuf.at[r], nv_hbm.at[r, :, 0], nvsem.at[r]).start()
 
+
+    def raw_scores(r):
+        ctx = ctx_ref[r]
+        rows = pl.ds(pl.multiple_of(r * TREE, 8), TREE)
         lane = lax.broadcasted_iota(jnp.int32, (TREE, NBLK * BLK), 1)
         pos = (lane // BLK * CP + cp_rank) * BLK + lane % BLK - ctx
         onehot = (pos == lax.broadcasted_iota(jnp.int32, (TREE, NBLK * BLK), 0)).astype(jnp.bfloat16)
@@ -165,12 +180,17 @@
 
         stats = jnp.zeros((TREE, HEAD), jnp.float32)
         stat_lane = lax.broadcasted_iota(jnp.int32, (TREE, HEAD), 1)
+        scores = []
         for hd in range(KV):
             query = qkv[hd * GROUP:(hd + 1) * GROUP, rows, :].reshape(GROUP * TREE, HEAD).astype(jnp.bfloat16)
             keys = kbuf[r, :, hd].reshape(NBLK * BLK, HEAD)
+            scores.append(lax.dot_general(query, keys, (((1,), (1,)), ((), ())), preferred_element_type=jnp.float32))
+        return bias, stats, stat_lane, scores
+
+    def finish(r, bias, stats, stat_lane, scores):
+        for hd in range(KV):
             vals = vbuf[r, :, hd].reshape(NBLK * BLK, HEAD)
-            score = lax.dot_general(query, keys, (((1,), (1,)), ((), ())), preferred_element_type=jnp.float32)
-            score = score.reshape(GROUP, TREE, NBLK * BLK) * (HEAD ** -0.5 * LOG2E) + bias[None]
+            score = scores[hd].reshape(GROUP, TREE, NBLK * BLK) * (HEAD ** -0.5 * LOG2E) + bias[None]
             top = jnp.max(score, axis=-1, keepdims=True)
             prob = jnp.exp2(score - top)
             total = jnp.sum(prob, axis=-1, keepdims=True)
@@ -181,9 +201,24 @@
                 stats = jnp.where(stat_lane == head, top[g], stats)
                 stats = jnp.where(stat_lane == HEADS + head, total[g], stats)
         o_ref[r, :, WIDE:] = stats
-        return carry
-
-    lax.fori_loop(0, REQ, attend_step, 0)
+
+
+    def attend_step(i, carry):
+        group = [i * UNROLL + k for k in range(UNROLL)]
+        for r in group:
+            prepare(r)
+        held = [raw_scores(r) for r in group]
+        for r, values in zip(group, held):
+            finish(r, *values)
+        return carry
+
+    lax.fori_loop(0, EARLY // UNROLL, attend_step, 0)
+
+    def rest(r, carry):
+        prepare(r)
+        return carry
+
+    lax.fori_loop(EARLY, REQ, rest, 0)
 
     def drain(r, carry):
         pltpu.make_async_copy(kbuf.at[r], nk_hbm.at[r, :, 0], nksem.at[r]).wait()
@@ -202,10 +237,10 @@
     return fa, fb, total, jnp.where(lane < HEADS, top, total)
 
 
-def tail_kernel(own, w_hbm, x_hbm, y_ref,
-                pin, yrecv, heads, hbf, wbuf, xbuf,
+def main_kernel(ctx_ref, mask_ref, qkv, early, k_hbm, v_hbm, w_hbm, x_hbm, y_ref,
+                kbuf, vbuf, late, pin, yrecv, heads, hbf, wbuf, xbuf,
                 part, in_end, in_mid, fin, fin_y, fin_c, fin_cy,
-                wsem, xsem, s_p, r_p, s_y, r_y, s_a, r_a,
+                ksem, vsem, wsem, xsem, s_p, r_p, s_y, r_y, s_a, r_a,
                 s_e, r_e, s_m, r_m, s_f, r_f, s_yf, r_yf, s_cf, r_cf, s_cy, r_cy):
     cp_rank = lax.axis_index('cp')
     z = lax.axis_index('tp')
@@ -230,6 +265,11 @@
     def _():
         pl.semaphore_signal(barrier, inc=1, device_id=middle, device_id_type=MESH)
 
+    for r in range(EARLY, REQ):
+        slot = r - EARLY
+        pltpu.make_async_copy(k_hbm.at[r, :, 0], kbuf.at[slot], ksem.at[slot]).start()
+        pltpu.make_async_copy(v_hbm.at[r, :, 0], vbuf.at[slot], vsem.at[slot]).start()
+
     def weight_copy(j):
         cols = pl.ds(pl.multiple_of(core * HALF + j * W, W), W)
         return pltpu.make_async_copy(w_hbm.at[:, cols], wbuf.at[j], wsem.at[j])
@@ -238,26 +278,60 @@
         weight_copy(j).start()
         return carry
 
-    lax.fori_loop(0, NP, start_weight, 0)
     x_copies = [pltpu.make_async_copy(
         x_hbm.at[pl.ds(pl.multiple_of(w * WAVE_ROWS + yy * PART_ROWS, 16), PART_ROWS), pl.ds(pl.multiple_of(core * HALF, HALF), HALF)],
         xbuf.at[w], xsem.at[w]) for w in range(WAVES)]
-    for copy in x_copies:
-        copy.start()
-
-    @pl.when(mid == 1)
-    def _():
-        pl.semaphore_wait(barrier, 4)
-
-    @pl.when(mid == 0)
-    def _():
-        pl.semaphore_wait(barrier, 3)
+    def raw_scores(r):
+        slot = r - EARLY
+        ctx = ctx_ref[r]
+        rows = pl.ds(pl.multiple_of(r * TREE, 8), TREE)
+        lane = lax.broadcasted_iota(jnp.int32, (TREE, NBLK * BLK), 1)
+        pos = (lane // BLK * CP + cp_rank) * BLK + lane % BLK - ctx
+        onehot = (pos == lax.broadcasted_iota(jnp.int32, (TREE, NBLK * BLK), 0)).astype(jnp.bfloat16)
+        allowed = jnp.dot(mask_ref[r].astype(jnp.float32).astype(jnp.bfloat16), onehot, preferred_element_type=jnp.float32)
+        bias = jnp.where((pos < 0) | (allowed > 0.5), 0.0, MASKED)
+        scores = []
+        for hd in range(KV):
+            query = qkv[hd * GROUP:(hd + 1) * GROUP, rows, :].reshape(GROUP * TREE, HEAD).astype(jnp.bfloat16)
+            keys = kbuf[slot, :, hd].reshape(NBLK * BLK, HEAD)
+            scores.append(lax.dot_general(query, keys, (((1,), (1,)), ((), ())), preferred_element_type=jnp.float32))
+        return bias, scores
+
+    def attend(r, bias, scores):
+        slot = r - EARLY
+        stats = jnp.zeros((TREE, HEAD), jnp.float32)
+        stat_lane = lax.broadcasted_iota(jnp.int32, (TREE, HEAD), 1)
+        for hd in range(KV):
+            vals = vbuf[slot, :, hd].reshape(NBLK * BLK, HEAD)
+            score = scores[hd].reshape(GROUP, TREE, NBLK * BLK) * (HEAD ** -0.5 * LOG2E) + bias[None]
+            top = jnp.max(score, axis=-1, keepdims=True)
+            prob = jnp.exp2(score - top)
+            total = jnp.sum(prob, axis=-1, keepdims=True)
+            mixed = jnp.dot(prob.reshape(GROUP * TREE, NBLK * BLK).astype(jnp.bfloat16), vals, preferred_element_type=jnp.float32)
+            for g in range(GROUP):
+                head = hd * GROUP + g
+                late[slot, :, head * HEAD:(head + 1) * HEAD] = mixed[g * TREE:(g + 1) * TREE]
+                stats = jnp.where(stat_lane == head, top[g], stats)
+                stats = jnp.where(stat_lane == HEADS + head, total[g], stats)
+        late[slot, :, WIDE:] = stats
+
+    def enter():
+        @pl.when(mid == 1)
+        def _():
+            pl.semaphore_wait(barrier, 4)
+
+        @pl.when(mid == 0)
+        def _():
+            pl.semaphore_wait(barrier, 3)
+
+    def own(w, chip, to_core):
+        return late.at[2 * chip + to_core] if w == WAVES - 1 else early.at[4 * w + 2 * chip + to_core]
 
     def chip_copy(w, side):
         chip = yy if side else other_y
-        return remote(own.at[4 * w + 2 * chip + other_core], pin.at[w, side], s_p.at[w, side], r_p.at[w, side], partner)
-
-    for w in range(WAVES):
+        return remote(own(w, chip, other_core), pin.at[w, side], s_p.at[w, side], r_p.at[w, side], partner)
+
+    def exchange(w):
         for side in (0, 1):
             chip_copy(w, side).start()
 
@@ -289,35 +363,71 @@
         head_copy(w, other_core).wait_recv()
         hbf[...] = heads[w].reshape(PART_ROWS, WIDE).astype(jnp.bfloat16)
 
-    for w in range(WAVES):
+    def blend_across(w):
         chip_copy(w, 0).wait_recv()
-        blend(own.at[4 * w + 2 * other_y + core], pin.at[w, 0])
+        blend(own(w, other_y, core), pin.at[w, 0])
         y_copy(w).start()
-    for w in range(WAVES):
+
+    def blend_mine(w):
         chip_copy(w, 1).wait_recv()
-        blend(own.at[4 * w + 2 * yy + core], pin.at[w, 1])
+        blend(own(w, yy, core), pin.at[w, 1])
+
+    def pair_step(i, carry):
+        pair_of = [EARLY + UNROLL * i + k for k in range(UNROLL)]
+        for r in pair_of:
+            slot = r - EARLY
+            pltpu.make_async_copy(k_hbm.at[r, :, 0], kbuf.at[slot], ksem.at[slot]).wait()
+            pltpu.make_async_copy(v_hbm.at[r, :, 0], vbuf.at[slot], vsem.at[slot]).wait()
+
+        @pl.when(i == 0)
+        def _():
+            lax.fori_loop(0, NP, start_weight, 0)
+            for copy in x_copies:
+                copy.start()
+
+        held = [raw_scores(r) for r in pair_of]
+        for r, values in zip(pair_of, held):
+            attend(r, *values)
+
+        @pl.when(i == 0)
+        def _():
+            blend_across(0)
+
+        @pl.when(i == 1)
+        def _():
+            exchange(2)
+            blend_across(1)
+            blend_mine(0)
+            blend_mine(1)
+        return carry
+
+    enter()
+    exchange(0)
+    exchange(1)
+    lax.fori_loop(0, LATE // UNROLL, pair_step, 0)
     for copy in x_copies:
         copy.wait()
     finish_start(0)
+    blend_across(2)
     finish_end(0)
 
     def end_copy(p):
-        return remote(part.at[p], in_end.at[p], s_e.at[p], r_e.at[p], pair)
+        return remote(part.at[p], in_end.at[p], s_e, r_e.at[p], pair)
 
     def mid_copy(p):
-        return remote(part.at[p], in_mid.at[p], s_m.at[p], r_m.at[p], middle)
+        return remote(part.at[p], in_mid.at[p], s_m, r_m.at[p], middle)
 
     def fin_copy(p):
-        return remote(fin.at[p], fin.at[p], s_f.at[p], r_f.at[p], pair)
+        return remote(fin.at[p], fin.at[p], s_f, r_f.at[p], pair)
 
     def across_copy(p):
-        return remote(fin.at[p], fin_y.at[p], s_yf.at[p], r_yf.at[p], across)
+        return remote(fin.at[p], fin_y.at[p], s_yf, r_yf.at[p], across)
 
     def core_copy(p):
-        return remote(fin.at[p], fin_c.at[p], s_cf.at[p], r_cf.at[p], partner)
+        return remote(fin.at[p], fin_c.at[p], s_cf, r_cf.at[p], partner)
 
     def core_y_copy(p):
-        return remote(fin_y.at[p], fin_cy.at[p], s_cy.at[p], r_cy.at[p], partner)
+        return remote(fin_y.at[p], fin_cy.at[p], s_cy, r_cy.at[p], partner)
 
     def project(p):
         j = p % NP
@@ -376,8 +486,9 @@
         return carry
 
     lax.fori_loop(0, AHEAD, ahead_step, 0)
+    blend_mine(2)
     lag = lambda at_mid, at_end: jnp.where(mid == 1, at_mid, at_end)
-    lag_core, lag_across, lag_core_y = lag(6, 9), lag(8, 11), lag(10, 13)
+    lag_core, lag_across, lag_core_y = lag(5, 8), lag(7, 10), lag(9, 12)
 
     def step(s, carry):
         for w in range(1, WAVES):
@@ -397,13 +508,13 @@
         def _():
             take_end(s)
 
-        @pl.when((mid == 1) & (s >= 4) & (s < PIECES + 4))
-        def _():
-            take_mid(s - 4)
-
-        @pl.when((mid == 0) & (s >= 7) & (s < PIECES + 7))
-        def _():
-            take_fin(s - 7)
+        @pl.when((mid == 1) & (s >= 3) & (s < PIECES + 3))
+        def _():
+            take_mid(s - 3)
+
+        @pl.when((mid == 0) & (s >= 6) & (s < PIECES + 6))
+        def _():
+            take_fin(s - 6)
 
         for this_lag, body in ((lag_core, take_core), (lag_across, take_across), (lag_core_y, take_core_y)):
             p = s - this_lag
@@ -413,7 +524,7 @@
                 body(p)
         return carry
 
-    lax.fori_loop(0, PIECES + 13, step, 0)
+    lax.fori_loop(0, PIECES + 12, step, 0)
 
     for w in range(WAVES):
         for side in (0, 1):
@@ -421,22 +532,18 @@
         y_copy(w).wait_send()
         head_copy(w, core).wait_send()
 
-    def sent(p, carry):
-        across_copy(p).wait_send()
-        core_copy(p).wait_send()
-        core_y_copy(p).wait_send()
-
-        @pl.when(mid == 1)
-        def _():
-            mid_copy(p).wait_send()
-            fin_copy(p).wait_send()
-
-        @pl.when(mid == 0)
-        def _():
-            end_copy(p).wait_send()
-        return carry
-
-    lax.fori_loop(0, PIECES, sent, 0)
+    remote(fin, fin_y, s_yf, r_yf.at[0], across).wait_send()
+    remote(fin, fin_c, s_cf, r_cf.at[0], partner).wait_send()
+    remote(fin_y, fin_cy, s_cy, r_cy.at[0], partner).wait_send()
+
+    @pl.when(mid == 1)
+    def _():
+        remote(part, in_mid, s_m, r_m.at[0], middle).wait_send()
+        remote(fin, fin, s_f, r_f.at[0], pair).wait_send()
+
+    @pl.when(mid == 0)
+    def _():
+        remote(part, in_end, s_e, r_e.at[0], pair).wait_send()
 
 
 def solution(mesh):
@@ -452,37 +559,37 @@
         cos_tab, sin_tab = rope_tables(positions)
         flat = hidden.reshape(ROWS, D)
         cache_shape = jax.ShapeDtypeStruct(cache_k.shape, bf16)
-        partial_out, new_k, new_v = pl.pallas_call(
+        early_out, heads_qkv, new_k, new_v = pl.pallas_call(
             attend_kernel,
-            out_shape=(pltpu.VMEM((REQ, TREE, EXT), f32), cache_shape, cache_shape),
+            out_shape=(pltpu.VMEM((EARLY, TREE, EXT), f32), pltpu.VMEM((HEADS + 2 * KV, ROWS, HEAD), f32), cache_shape, cache_shape),
             in_specs=[smem, vmem, vmem, vmem, vmem] + [anywhere] * 6,
-            out_specs=(vmem, anywhere, anywhere),
+            out_specs=(vmem, vmem, anywhere, anywhere),
             scratch_shapes=[
                 pltpu.VMEM((ROWS, D), bf16), pltpu.VMEM((ROWS, D), bf16), pltpu.VMEM((2, ROWS, HEAD), f32), pltpu.VMEM((RING, D, TILE), bf16),
-                pltpu.VMEM((HEADS + 2 * KV, ROWS, HEAD), f32),
                 pltpu.VMEM((REQ, NBLK, KV, BLK, HEAD), bf16), pltpu.VMEM((REQ, NBLK, KV, BLK, HEAD), bf16),
-                dma, dma((RING,)), dma((REQ,)), dma((REQ,)), dma((REQ,)), dma((REQ,)),
+                dma((XCHUNKS,)), dma((RING,)), dma((REQ,)), dma((REQ,)), dma((REQ,)), dma((REQ,)),
             ],
-            compiler_params=pltpu.CompilerParams(vmem_limit_bytes=56 * 1024 * 1024),
-            cost_estimate=pl.CostEstimate(flops=20_000_000_000, bytes_accessed=72_000_000, transcendentals=5_000_000),
+            compiler_params=pltpu.CompilerParams(vmem_limit_bytes=54 * 1024 * 1024),
+            cost_estimate=pl.CostEstimate(flops=15_000_000_000, bytes_accessed=72_000_000, transcendentals=4_000_000),
             name='attend',
         )(ctx_len, attn_gain, pltpu.with_memory_space_constraint(cos_tab, pltpu.VMEM), pltpu.with_memory_space_constraint(sin_tab, pltpu.VMEM), tree_mask, flat, w_query, w_key, w_value, cache_k, cache_v)
         pieces = pltpu.VMEM((PIECES, PART_ROWS, W), f32)
         out = pl.pallas_call(
-            tail_kernel,
+            main_kernel,
             out_shape=pltpu.VMEM((ROWS, D), bf16),
-            in_specs=[vmem, anywhere, anywhere],
+            in_specs=[smem, vmem, vmem, vmem] + [anywhere] * 4,
             out_specs=vmem,
             scratch_shapes=[
-                pltpu.VMEM((WAVES, 2, TREE, EXT), f32), pltpu.VMEM((WAVES, TREE, EXT), f32), pltpu.VMEM((WAVES, 2, TREE, WIDE), f32),
+                pltpu.VMEM((LATE, NBLK, KV, BLK, HEAD), bf16), pltpu.VMEM((LATE, NBLK, KV, BLK, HEAD), bf16),
+                pltpu.VMEM((LATE, TREE, EXT), f32), pltpu.VMEM((WAVES, 2, TREE, EXT), f32), pltpu.VMEM((WAVES, TREE, EXT), f32), pltpu.VMEM((WAVES, 2, TREE, WIDE), f32),
                 pltpu.VMEM((PART_ROWS, WIDE), bf16), pltpu.VMEM((NP, WIDE, W), bf16), pltpu.VMEM((WAVES, PART_ROWS, HALF), bf16),
                 pieces, pieces, pieces, pieces, pieces, pieces, pieces,
-                dma((NP,)), dma((WAVES,)), dma((WAVES, 2)), dma((WAVES, 2)), dma((WAVES,)), dma((WAVES,)), dma((WAVES,)), dma((WAVES,)),
-            ] + [dma((PIECES,)) for _ in range(12)],
-            compiler_params=pltpu.CompilerParams(vmem_limit_bytes=48 * 1024 * 1024, collective_id=0, has_side_effects=True),
-            cost_estimate=pl.CostEstimate(flops=2_500_000_000, bytes_accessed=30_000_000, transcendentals=100_000),
-            name='tail',
-        )(pltpu.with_memory_space_constraint(partial_out, pltpu.VMEM), w_out, flat)
+                dma((LATE,)), dma((LATE,)), dma((NP,)), dma((WAVES,)), dma((WAVES, 2)), dma((WAVES, 2)), dma((WAVES,)), dma((WAVES,)), dma((WAVES,)), dma((WAVES,)),
+            ] + [dma, dma((PIECES,))] * 6,
+            compiler_params=pltpu.CompilerParams(vmem_limit_bytes=50 * 1024 * 1024, collective_id=0, has_side_effects=True),
+            cost_estimate=pl.CostEstimate(flops=5_000_000_000, bytes_accessed=42_000_000, transcendentals=5_000_000),
+            name='main',
+        )(ctx_len, tree_mask, pltpu.with_memory_space_constraint(heads_qkv, pltpu.VMEM), pltpu.with_memory_space_constraint(early_out, pltpu.VMEM), new_k, new_v, w_out, flat)
         return out.reshape(REQ, TREE, D), new_k, new_v
 
     return jax.shard_map(local_step, mesh=mesh, in_specs=(row_spec, P(), P(None, 'tp'), P(None, 'tp'), P(None, 'tp'), P('tp', None), cache_spec, cache_spec, row_spec, row_spec, row_spec), out_specs=(row_spec, cache_spec, cache_spec), check_vma=False)

time: 123 us -> 115 us (0.935)
  Pallas kernels: 119 us -> 110 us
    pallas_call x2, Pallas kernels: 119 us -> 110 us  [the longest x1 81.5 us: local_step(): pl.pallas_call(main_kernel, out_shape=pltpu.VMEM((ROWS, D), bf16), in_spe...]
where the time goes in v3:
time: 115 us
  Pallas kernels  110 us (96%)
  local copies, waits for them, and re-layouts  2.27 us (2%)
  other arithmetic  1.31 us (1%)
    pallas_call x1, Pallas kernels, local_step(): pl.pallas_call(main_kernel, out_shape=pltpu.VMEM((ROWS, D), bf16), in_spe...  81.5 us
    pallas_call x1, Pallas kernels, local_step(): pl.pallas_call(attend_kernel, out_shape=(pltpu.VMEM((EARLY, TREE, EXT), f...  29 us

profile of v3, /device:TPU:0, one launch (start us, length us, event | category | flops | bytes accessed | tf_op | source)
XLA Modules:
  0.0 114.7 jit_solution(8705903225465991980)
XLA Ops:
  0.7 0.7 convert_element_type.3
  1.4 0.1 mul.33
  1.4 0.6 multiply_sine_fusion
  2.0 29.0 %attend.1 = (f32[8,24,2176]{2,1,0:T(8,128)S(1)}, f32[20,288,128]{2,1,0:T(8,128)S(1)}, bf16[12,4,1,2,256,128]{5,4,3,2,1,0:T(8,128)(2,1)}, bf16[12,4,1,2,256,128]{5,4,3,2,1,0:T(8,128)(2,1)}) custom-call(s32[12]{0:T(128)} %ctx_ref.3, bf16[8192]{0:T(1024)(128)(2,1)} %gain_ref.1, f32[288,64]{1,0:T(8,128)S(1)} %get-tuple-element.12.cos_ref, ...), custom_call_target="tpu_custom_call" | custom-call | flops 15000000512 | bytes 72000000 | tf_op jit(solution)/shard_map/attend/pallas_call | solution.py:562
  31.0 81.5 %main.1 = bf16[288,8192]{1,0:T(8,128)(2,1)S(1)} custom-call(s32[12]{0:T(128)} %ctx_ref.3, s32[12,24,24]{2,1,0:T(8,128)} %mask_ref.3, f32[20,288,128]{2,1,0:T(8,128)S(1)} %get-tuple-element.7.qkv, f32[8,24,2176]{2,1,0:T(8,128)S(1)} %get-tuple-element.8.early, bf16[12,4,1,2,256,128]{5,4,3,2,1,0:T(8,128)(2,1)} %get-tuple-element.17.k_hbm, ...), custom_call_target="tpu_custom_call" | custom-call | flops 5000000000 | bytes 42000000 | tf_op jit(solution)/shard_map/main/pallas_call | solution.py:577
  112.5 2.2 %copy.15 = bf16[12,24,8192]{2,1,0:T(8,128)(2,1)} copy(bf16[12,24,8192]{2,1,0:T(8,128)(2,1)S(1)} %bitcast.2) | data formatting | bytes 9437184
  (1 shorter events, 0.0 us)

commit v4 on v3

--- a/solution.py
+++ b/solution.py
@@ -27,10 +27,9 @@
 WIDE = HEADS * HEAD
 EXT = WIDE + HEAD
 TILE = 256
-NTILE = (HEADS + 2 * KV) * HEAD // TILE
-RING = 4
+NTILE = (HEADS + 2 * KV) * HEAD // TILE // 2
 XCHUNKS = 3
-CACHE_AHEAD = 8
+STEPS_AHEAD = 2
 EARLY = 8
 LATE = REQ - EARLY
 HALF = D // 2
@@ -54,37 +53,29 @@
     return jnp.cos(angle).reshape(ROWS, HEAD // 2), jnp.sin(angle).reshape(ROWS, HEAD // 2)
 
 
-def attend_kernel(ctx_ref, gain_ref, cos_ref, sin_ref, mask_ref, x_hbm, wq_hbm, wk_hbm, wv_hbm, ck_hbm, cv_hbm,
-                  o_ref, qkv, nk_hbm, nv_hbm,
-                  x_ref, h_ref, turn, wbuf, kbuf, vbuf, xsem, wsem, ksem, vsem, nksem, nvsem):
+def project_kernel(cos_ref, sin_ref, gain_hbm, x_hbm, wq_hbm, wk_hbm, wv_hbm, qkv,
+                   x_ref, gain_ref, h_ref, turn, wbuf, xsem, gsem, wsem, s_q, r_q):
     cp_rank = lax.axis_index('cp')
-    nq = HEADS * HEAD // TILE
+    core = cp_rank % 2
+    partner = {'cp': cp_rank + 1 - 2 * core}
 
     x_copies = []
     for k in range(XCHUNKS):
         rows = pl.ds(k * (ROWS // XCHUNKS), ROWS // XCHUNKS)
         x_copies.append(pltpu.make_async_copy(x_hbm.at[rows, :], x_ref.at[rows, :], xsem.at[k]))
         x_copies[k].start()
-
-    def start_weight(i):
-        slot = lax.rem(i, RING)
-
-        @pl.when(i < nq)
-        def _():
-            cols = pl.ds(pl.multiple_of(i * TILE, TILE), TILE)
-            pltpu.make_async_copy(wq_hbm.at[:, cols], wbuf.at[slot], wsem.at[slot]).start()
-
-        @pl.when(i == nq)
-        def _():
-            pltpu.make_async_copy(wk_hbm, wbuf.at[slot], wsem.at[slot]).start()
-
-        @pl.when(i == nq + 1)
-        def _():
-            pltpu.make_async_copy(wv_hbm, wbuf.at[slot], wsem.at[slot]).start()
-
-    def start_cache(r):
-        pltpu.make_async_copy(ck_hbm.at[r, :, 0], kbuf.at[r], ksem.at[r]).start()
-        pltpu.make_async_copy(cv_hbm.at[r, :, 0], vbuf.at[r], vsem.at[r]).start()
+    gain_copy = pltpu.make_async_copy(gain_hbm, gain_ref, gsem)
+    gain_copy.start()
+    barrier = pltpu.get_barrier_semaphore()
+    pl.semaphore_signal(barrier, inc=1, device_id=partner, device_id_type=MESH)
+
+    def start_weights():
+        one = pl.ds(pl.multiple_of(core * HEAD, HEAD), HEAD)
+        pltpu.make_async_copy(wk_hbm.at[:, one], wbuf.at[0, :, :HEAD], wsem.at[0]).start()
+        pltpu.make_async_copy(wv_hbm.at[:, one], wbuf.at[0, :, HEAD:], wsem.at[0]).start()
+        for i in range(1, NTILE):
+            cols = pl.ds(pl.multiple_of(core * (WIDE // 2) + (i - 1) * TILE, TILE), TILE)
+            pltpu.make_async_copy(wq_hbm.at[:, cols], wbuf.at[i], wsem.at[i]).start()
 
     turn[0] = jnp.concatenate([cos_ref[...], cos_ref[...]], axis=-1)
     turn[1] = jnp.concatenate([-sin_ref[...], sin_ref[...]], axis=-1)
@@ -101,42 +92,57 @@
             h_ref[rows, cols] = (wide * inv * gain_ref[cols].astype(jnp.float32).reshape(1, HEAD)).astype(jnp.bfloat16)
         return carry
 
+    gain_copy.wait()
     for k in range(XCHUNKS):
         x_copies[k].wait()
         if k == 0:
-            for i in range(RING):
-                start_weight(jnp.int32(i))
+            start_weights()
         lax.fori_loop(k * (ROWS // 16 // XCHUNKS), (k + 1) * (ROWS // 16 // XCHUNKS), norm_step, 0)
+    pl.semaphore_wait(barrier, 1)
+
+    def head_copy(head, n):
+        return pltpu.make_async_remote_copy(src_ref=qkv.at[head], dst_ref=qkv.at[head], send_sem=s_q, recv_sem=r_q.at[n], device_id=partner, device_id_type=MESH)
 
     def proj_step(i, carry):
-        slot = lax.rem(i, RING)
-        pltpu.make_async_copy(wq_hbm.at[:, :TILE], wbuf.at[slot], wsem.at[slot]).wait()
-        acc = jnp.dot(h_ref[...], wbuf[slot], preferred_element_type=jnp.float32)
-        for hh in range(TILE // HEAD):
+        pltpu.make_async_copy(wq_hbm.at[:, :TILE], wbuf.at[i], wsem.at[i]).wait()
+        acc = jnp.dot(h_ref[...], wbuf[i], preferred_element_type=jnp.float32)
+        for hh in range(2):
             part = acc[:, hh * HEAD:(hh + 1) * HEAD]
             turned = pltpu.roll(part, HEAD // 2, 1)
             cos_tab, sin_tab = turn[0], turn[1]
-            cos_tab = jnp.where(i < NTILE - 1, cos_tab, 1.0)
-            sin_tab = jnp.where(i < NTILE - 1, sin_tab, 0.0)
-            qkv[(TILE // HEAD) * i + hh] = part * cos_tab + turned * sin_tab
-
-        @pl.when(i + RING < NTILE)
-        def _():
-            start_weight(i + RING)
-
-        @pl.when(i + RING >= NTILE)
-        def _():
-            for k in range(CACHE_AHEAD // RING):
-                start_cache((i + RING - NTILE) * (CACHE_AHEAD // RING) + k)
+            if hh == 1:
+                cos_tab = jnp.where(i > 0, cos_tab, 1.0)
+                sin_tab = jnp.where(i > 0, sin_tab, 0.0)
+            head = jnp.where(i == 0, HEADS + KV * hh + core, GROUP * core + 2 * (i - 1) + hh)
+            qkv[head] = part * cos_tab + turned * sin_tab
+            head_copy(head, 2 * i + hh).start()
         return carry
 
     lax.fori_loop(0, NTILE, proj_step, 0)
+    for n in range(2 * NTILE):
+        head_copy(0, n).wait_recv()
+    half = qkv.at[pl.ds(0, 2 * NTILE)]
+    pltpu.make_async_remote_copy(src_ref=half, dst_ref=half, send_sem=s_q, recv_sem=r_q.at[0], device_id=partner, device_id_type=MESH).wait_send()
+
+
+def attend_kernel(ctx_ref, mask_ref, qkv, ck_hbm, cv_hbm,
+                  o_ref, nk_hbm, nv_hbm,
+                  kbuf, vbuf, ksem, vsem, nksem, nvsem):
+    cp_rank = lax.axis_index('cp')
+
+    def start_cache(r):
+        pltpu.make_async_copy(ck_hbm.at[r, :, 0], kbuf.at[r], ksem.at[r]).start()
+        pltpu.make_async_copy(cv_hbm.at[r, :, 0], vbuf.at[r], vsem.at[r]).start()
+
+    def start_step(i):
+        for k in range(UNROLL):
+            start_cache(UNROLL * i + k)
+        start_cache(EARLY + i)
+
+    for i in range(STEPS_AHEAD):
+        start_step(i)
 
     def prepare(r):
-        @pl.when(r + CACHE_AHEAD < REQ)
-        def _():
-            start_cache(r + CACHE_AHEAD)
-
         pltpu.make_async_copy(ck_hbm.at[r, :, 0], kbuf.at[r], ksem.at[r]).wait()
         pltpu.make_async_copy(cv_hbm.at[r, :, 0], vbuf.at[r], vsem.at[r]).wait()
         ctx = ctx_ref[r]
@@ -204,21 +210,20 @@
 
 
     def attend_step(i, carry):
+        @pl.when(i + STEPS_AHEAD < EARLY // UNROLL)
+        def _():
+            start_step(i + STEPS_AHEAD)
+
         group = [i * UNROLL + k for k in range(UNROLL)]
         for r in group:
             prepare(r)
         held = [raw_scores(r) for r in group]
         for r, values in zip(group, held):
             finish(r, *values)
+        prepare(EARLY + i)
         return carry
 
     lax.fori_loop(0, EARLY // UNROLL, attend_step, 0)
-
-    def rest(r, carry):
-        prepare(r)
-        return carry
-
-    lax.fori_loop(EARLY, REQ, rest, 0)
 
     def drain(r, carry):
         pltpu.make_async_copy(kbuf.at[r], nk_hbm.at[r, :, 0], nksem.at[r]).wait()
@@ -488,7 +493,7 @@
     lax.fori_loop(0, AHEAD, ahead_step, 0)
     blend_mine(2)
     lag = lambda at_mid, at_end: jnp.where(mid == 1, at_mid, at_end)
-    lag_core, lag_across, lag_core_y = lag(5, 8), lag(7, 10), lag(9, 12)
+    lag_core, lag_across, lag_core_y = lag(6, 9), lag(8, 11), lag(10, 13)
 
     def step(s, carry):
         for w in range(1, WAVES):
@@ -512,9 +517,9 @@
         def _():
             take_mid(s - 3)
 
-        @pl.when((mid == 0) & (s >= 6) & (s < PIECES + 6))
-        def _():
-            take_fin(s - 6)
+        @pl.when((mid == 0) & (s >= 7) & (s < PIECES + 7))
+        def _():
+            take_fin(s - 7)
 
         for this_lag, body in ((lag_core, take_core), (lag_across, take_across), (lag_core_y, take_core_y)):
             p = s - this_lag
@@ -524,7 +529,7 @@
                 body(p)
         return carry
 
-    lax.fori_loop(0, PIECES + 12, step, 0)
+    lax.fori_loop(0, PIECES + 13, step, 0)
 
     for w in range(WAVES):
         for side in (0, 1):
@@ -559,20 +564,33 @@
         cos_tab, sin_tab = rope_tables(positions)
         flat = hidden.reshape(ROWS, D)
         cache_shape = jax.ShapeDtypeStruct(cache_k.shape, bf16)
-        early_out, heads_qkv, new_k, new_v = pl.pallas_call(
+        heads_qkv = pl.pallas_call(
+            project_kernel,
+            out_shape=pltpu.VMEM((HEADS + 2 * KV, ROWS, HEAD), f32),
+            in_specs=[vmem, vmem, pl.BlockSpec(memory_space=pltpu.HBM)] + [anywhere] * 4,
+            out_specs=vmem,
+            scratch_shapes=[
+                pltpu.VMEM((ROWS, D), bf16), pltpu.VMEM((D,), bf16), pltpu.VMEM((ROWS, D), bf16), pltpu.VMEM((2, ROWS, HEAD), f32), pltpu.VMEM((NTILE, D, TILE), bf16),
+                dma((XCHUNKS,)), dma, dma((NTILE,)), dma, dma((2 * NTILE,)),
+            ],
+            compiler_params=pltpu.CompilerParams(vmem_limit_bytes=50 * 1024 * 1024, collective_id=1, has_side_effects=True),
+            cost_estimate=pl.CostEstimate(flops=6_000_000_000, bytes_accessed=26_000_000, transcendentals=1_000),
+            name='project',
+        )(pltpu.with_memory_space_constraint(cos_tab, pltpu.VMEM), pltpu.with_memory_space_constraint(sin_tab, pltpu.VMEM), pltpu.with_memory_space_constraint(attn_gain, pltpu.HBM), flat, w_query, w_key, w_value)
+        heads_qkv = pltpu.with_memory_space_constraint(heads_qkv, pltpu.VMEM)
+        early_out, new_k, new_v = pl.pallas_call(
             attend_kernel,
-            out_shape=(pltpu.VMEM((EARLY, TREE, EXT), f32), pltpu.VMEM((HEADS + 2 * KV, ROWS, HEAD), f32), cache_shape, cache_shape),
-            in_specs=[smem, vmem, vmem, vmem, vmem] + [anywhere] * 6,
-            out_specs=(vmem, vmem, anywhere, anywhere),
+            out_shape=(pltpu.VMEM((EARLY, TREE, EXT), f32), cache_shape, cache_shape),
+            in_specs=[smem, vmem, vmem] + [anywhere] * 2,
+            out_specs=(vmem, anywhere, anywhere),
             scratch_shapes=[
-                pltpu.VMEM((ROWS, D), bf16), pltpu.VMEM((ROWS, D), bf16), pltpu.VMEM((2, ROWS, HEAD), f32), pltpu.VMEM((RING, D, TILE), bf16),
                 pltpu.VMEM((REQ, NBLK, KV, BLK, HEAD), bf16), pltpu.VMEM((REQ, NBLK, KV, BLK, HEAD), bf16),
-                dma((XCHUNKS,)), dma((RING,)), dma((REQ,)), dma((REQ,)), dma((REQ,)), dma((REQ,)),
+                dma((REQ,)), dma((REQ,)), dma((REQ,)), dma((REQ,)),
             ],
-            compiler_params=pltpu.CompilerParams(vmem_limit_bytes=54 * 1024 * 1024),
-            cost_estimate=pl.CostEstimate(flops=15_000_000_000, bytes_accessed=72_000_000, transcendentals=4_000_000),
+            compiler_params=pltpu.CompilerParams(vmem_limit_bytes=40 * 1024 * 1024),
+            cost_estimate=pl.CostEstimate(flops=3_000_000_000, bytes_accessed=26_000_000, transcendentals=4_000_000),
             name='attend',
-        )(ctx_len, attn_gain, pltpu.with_memory_space_constraint(cos_tab, pltpu.VMEM), pltpu.with_memory_space_constraint(sin_tab, pltpu.VMEM), tree_mask, flat, w_query, w_key, w_value, cache_k, cache_v)
+        )(ctx_len, tree_mask, heads_qkv, cache_k, cache_v)
         pieces = pltpu.VMEM((PIECES, PART_ROWS, W), f32)
         out = pl.pallas_call(
             main_kernel,
@@ -589,7 +607,7 @@
             compiler_params=pltpu.CompilerParams(vmem_limit_bytes=50 * 1024 * 1024, collective_id=0, has_side_effects=True),
             cost_estimate=pl.CostEstimate(flops=5_000_000_000, bytes_accessed=42_000_000, transcendentals=5_000_000),
             name='main',
-        )(ctx_len, tree_mask, pltpu.with_memory_space_constraint(heads_qkv, pltpu.VMEM), pltpu.with_memory_space_constraint(early_out, pltpu.VMEM), new_k, new_v, w_out, flat)
+        )(ctx_len, tree_mask, heads_qkv, pltpu.with_memory_space_constraint(early_out, pltpu.VMEM), new_k, new_v, w_out, flat)
         return out.reshape(REQ, TREE, D), new_k, new_v
 
     return jax.shard_map(local_step, mesh=mesh, in_specs=(row_spec, P(), P(None, 'tp'), P(None, 'tp'), P(None, 'tp'), P('tp', None), cache_spec, cache_spec, row_spec, row_spec, row_spec), out_specs=(row_spec, cache_spec, cache_spec), check_vma=False)

time: 115 us -> 111 us (0.965)
  Pallas kernels: 110 us -> 106 us
    pallas_call x1, Pallas kernels: 29 us -> 10.4 us  [local_step(): pl.pallas_call(attend_kernel, out_shape=(pltpu.VMEM((EARLY, TREE, EXT), f...]
    pallas_call x0 -> x1, Pallas kernels: none -> 14.7 us  [local_step(): pl.pallas_call(project_kernel, out_shape=pltpu.VMEM((HEADS + 2 * KV, ROWS...]
where the time goes in v4:
time: 111 us; the launch traced here: 110 us
  Pallas kernels  106 us (95%)
  local copies, waits for them, and re-layouts  2.29 us (2%)
  other arithmetic  1.31 us (1%)
    pallas_call x1, Pallas kernels, local_step(): pl.pallas_call(main_kernel, out_shape=pltpu.VMEM((ROWS, D), bf16), in_spe...  81.1 us
    pallas_call x1, Pallas kernels, local_step(): pl.pallas_call(project_kernel, out_shape=pltpu.VMEM((HEADS + 2 * KV, ROWS...  14.7 us
    pallas_call x1, Pallas kernels, local_step(): pl.pallas_call(attend_kernel, out_shape=(pltpu.VMEM((EARLY, TREE, EXT), f...  10.4 us

profile of v4, /device:TPU:0, one launch (start us, length us, event | category | flops | bytes accessed | tf_op | source)
XLA Modules:
  0.0 110.5 jit_solution(14757999066941433260)
XLA Ops:
  0.7 0.7 convert_element_type.3
  1.4 0.1 mul.33
  1.4 0.6 multiply_sine_fusion
  2.0 0.0 copy-start
  2.0 0.0 copy-start.1
  2.1 0.0 copy-start.2
  2.1 14.7 %project.1.qkv = f32[20,288,128]{2,1,0:T(8,128)S(1)} custom-call(f32[288,64]{1,0:T(8,128)S(1)} %get-tuple-element.10.cos_ref, f32[288,64]{1,0:T(8,128)S(1)} %get-tuple-element.9.sin_ref, bf16[8192]{0:T(1024)(128)(2,1)} %gain_hbm.1, bf16[288,8192]{1,0:T(8,128)(2,1)} %bitcast.3, bf16[8192,2048]{1,0:T(8,128)(2,1)} %wq_hbm.1, bf16[8192,256]{1,0:T(8,128)(2,1)} %wk_hbm.1, ...), custom_call_target="tpu_custom_call" | custom-call | flops 6000000000 | bytes 26000000 | tf_op jit(solution)/shard_map/project/pallas_call | solution.py:567
  16.8 0.0 copy-done
  16.8 0.0 copy-done.1
  16.8 0.0 copy-done.2
  16.8 10.4 %attend.1 = (f32[8,24,2176]{2,1,0:T(8,128)S(1)}, bf16[12,4,1,2,256,128]{5,4,3,2,1,0:T(8,128)(2,1)}, bf16[12,4,1,2,256,128]{5,4,3,2,1,0:T(8,128)(2,1)}) custom-call(s32[12]{0:T(128)S(1)} %copy-done.2, s32[12,24,24]{2,1,0:T(8,128)S(1)} %copy-done.1, f32[20,288,128]{2,1,0:T(8,128)S(1)} %project.1.qkv, bf16[12,4,1,2,256,128]{5,4,3,2,1,0:T(8,128)(2,1)S(1)} %copy-done, ...), custom_call_target="tpu_custom_call" | custom-call | flops 3000000000 | bytes 26000000 | tf_op jit(solution)/shard_map/attend/pallas_call | solution.py:581
  27.2 81.1 %main.1 = bf16[288,8192]{1,0:T(8,128)(2,1)S(1)} custom-call(s32[12]{0:T(128)} %ctx_ref.3, s32[12,24,24]{2,1,0:T(8,128)} %mask_ref.3, f32[20,288,128]{2,1,0:T(8,128)S(1)} %project.1.qkv, f32[8,24,2176]{2,1,0:T(8,128)S(1)} %get-tuple-element.6.early, bf16[12,4,1,2,256,128]{5,4,3,2,1,0:T(8,128)(2,1)} %get-tuple-element.15.k_hbm, ...), custom_call_target="tpu_custom_call" | custom-call | flops 5000000000 | bytes 42000000 | tf_op jit(solution)/shard_map/main/pallas_call | solution.py:595
  108.3 2.2 %copy.15 = bf16[12,24,8192]{2,1,0:T(8,128)(2,1)} copy(bf16[12,24,8192]{2,1,0:T(8,128)(2,1)S(1)} %bitcast.2) | data formatting | bytes 9437184
  (1 shorter events, 0.0 us)
Async XLA Ops:
  2.0 14.7 %copy-start = (bf16[12,4,1,2,256,128]{5,4,3,2,1,0:T(8,128)(2,1)S(1)}, bf16[12,4,1,2,256,128]{5,4,3,2,1,0:T(8,128)(2,1)}, u32[]{:S(2)}) copy-start(bf16[12,4,1,2,256,128]{5,4,3,2,1,0:T(8,128)(2,1)} %ck_hbm.1) | copy-start | bytes 18874372
  2.0 14.7 %copy-start.1 = (s32[12,24,24]{2,1,0:T(8,128)S(1)}, s32[12,24,24]{2,1,0:T(8,128)}, u32[]{:S(2)}) copy-start(s32[12,24,24]{2,1,0:T(8,128)} %mask_ref.3) | copy-start | bytes 82948
  2.1 14.7 %copy-start.2 = (s32[12]{0:T(128)S(1)}, s32[12]{0:T(128)}, u32[]{:S(2)}) copy-start(s32[12]{0:T(128)} %ctx_ref.3) | copy-start | bytes 148

commit v5 on v4

--- a/solution.py
+++ b/solution.py
@@ -59,13 +59,13 @@
     core = cp_rank % 2
     partner = {'cp': cp_rank + 1 - 2 * core}
 
+    gain_copy = pltpu.make_async_copy(gain_hbm, gain_ref, gsem)
+    gain_copy.start()
     x_copies = []
     for k in range(XCHUNKS):
         rows = pl.ds(k * (ROWS // XCHUNKS), ROWS // XCHUNKS)
         x_copies.append(pltpu.make_async_copy(x_hbm.at[rows, :], x_ref.at[rows, :], xsem.at[k]))
         x_copies[k].start()
-    gain_copy = pltpu.make_async_copy(gain_hbm, gain_ref, gsem)
-    gain_copy.start()
     barrier = pltpu.get_barrier_semaphore()
     pl.semaphore_signal(barrier, inc=1, device_id=partner, device_id_type=MESH)
 

time: 111 us -> 110 us (level)
  no operation moved by 1% of the time
where the time goes in v5:
time: 110 us
  Pallas kernels  105 us (95%)
  local copies, waits for them, and re-layouts  2.29 us (2%)
  other arithmetic  1.31 us (1%)
    pallas_call x1, Pallas kernels, local_step(): pl.pallas_call(main_kernel, out_shape=pltpu.VMEM((ROWS, D), bf16), in_spe...  81.6 us
    pallas_call x1, Pallas kernels, local_step(): pl.pallas_call(project_kernel, out_shape=pltpu.VMEM((HEADS + 2 * KV, ROWS...  14.2 us
    pallas_call x1, Pallas kernels, local_step(): pl.pallas_call(attend_kernel, out_shape=(pltpu.VMEM((EARLY, TREE, EXT), f...  9.56 us
    unnamed x7, local copies, waits for them, and re-layouts  2.21 us

profile of v5, /device:TPU:0, one launch (start us, length us, event | category | flops | bytes accessed | tf_op | source)
XLA Modules:
  0.0 109.6 jit_solution(7934153443945749251)
XLA Ops:
  0.7 0.7 convert_element_type.3
  1.4 0.1 mul.33
  1.4 0.6 multiply_sine_fusion
  2.0 0.0 copy-start
  2.0 0.0 copy-start.1
  2.1 0.0 copy-start.2
  2.1 14.2 %project.1.qkv = f32[20,288,128]{2,1,0:T(8,128)S(1)} custom-call(f32[288,64]{1,0:T(8,128)S(1)} %get-tuple-element.10.cos_ref, f32[288,64]{1,0:T(8,128)S(1)} %get-tuple-element.9.sin_ref, bf16[8192]{0:T(1024)(128)(2,1)} %gain_hbm.1, bf16[288,8192]{1,0:T(8,128)(2,1)} %bitcast.3, bf16[8192,2048]{1,0:T(8,128)(2,1)} %wq_hbm.1, bf16[8192,256]{1,0:T(8,128)(2,1)} %wk_hbm.1, ...), custom_call_target="tpu_custom_call" | custom-call | flops 6000000000 | bytes 26000000 | tf_op jit(solution)/shard_map/project/pallas_call | solution.py:567
  16.3 0.0 copy-done
  16.3 0.0 copy-done.1
  16.3 0.0 copy-done.2
  16.3 9.6 %attend.1 = (f32[8,24,2176]{2,1,0:T(8,128)S(1)}, bf16[12,4,1,2,256,128]{5,4,3,2,1,0:T(8,128)(2,1)}, bf16[12,4,1,2,256,128]{5,4,3,2,1,0:T(8,128)(2,1)}) custom-call(s32[12]{0:T(128)S(1)} %copy-done.2, s32[12,24,24]{2,1,0:T(8,128)S(1)} %copy-done.1, f32[20,288,128]{2,1,0:T(8,128)S(1)} %project.1.qkv, bf16[12,4,1,2,256,128]{5,4,3,2,1,0:T(8,128)(2,1)S(1)} %copy-done, ...), custom_call_target="tpu_custom_call" | custom-call | flops 3000000000 | bytes 26000000 | tf_op jit(solution)/shard_map/attend/pallas_call | solution.py:581
  25.9 81.6 %main.1 = bf16[288,8192]{1,0:T(8,128)(2,1)S(1)} custom-call(s32[12]{0:T(128)} %ctx_ref.3, s32[12,24,24]{2,1,0:T(8,128)} %mask_ref.3, f32[20,288,128]{2,1,0:T(8,128)S(1)} %project.1.qkv, f32[8,24,2176]{2,1,0:T(8,128)S(1)} %get-tuple-element.6.early, bf16[12,4,1,2,256,128]{5,4,3,2,1,0:T(8,128)(2,1)} %get-tuple-element.15.k_hbm, ...), custom_call_target="tpu_custom_call" | custom-call | flops 5000000000 | bytes 42000000 | tf_op jit(solution)/shard_map/main/pallas_call | solution.py:595
  107.5 2.2 %copy.15 = bf16[12,24,8192]{2,1,0:T(8,128)(2,1)} copy(bf16[12,24,8192]{2,1,0:T(8,128)(2,1)S(1)} %bitcast.2) | data formatting | bytes 9437184
  (1 shorter events, 0.0 us)
Async XLA Ops:
  2.0 14.2 %copy-start = (bf16[12,4,1,2,256,128]{5,4,3,2,1,0:T(8,128)(2,1)S(1)}, bf16[12,4,1,2,256,128]{5,4,3,2,1,0:T(8,128)(2,1)}, u32[]{:S(2)}) copy-start(bf16[12,4,1,2,256,128]{5,4,3,2,1,0:T(8,128)(2,1)} %ck_hbm.1) | copy-start | bytes 18874372
  2.0 14.2 %copy-start.1 = (s32[12,24,24]{2,1,0:T(8,128)S(1)}, s32[12,24,24]{2,1,0:T(8,128)}, u32[]{:S(2)}) copy-start(s32[12,24,24]{2,1,0:T(8,128)} %mask_ref.3) | copy-start | bytes 82948
  2.1 14.2 %copy-start.2 = (s32[12]{0:T(128)S(1)}, s32[12]{0:T(128)}, u32[]{:S(2)}) copy-start(s32[12]{0:T(128)} %ctx_ref.3) | copy-start | bytes 148
